TPU v7x, 32 devices: a whole 2x2x4 slice. The times are simulated.
32 devices in a mesh: fsdp: 4 (over x, core), context: 2 (over y), tensor: 4 (over z).
Axes of the slice: x: 2, y: 2, z: 4, core: 2. Of those that a mesh axis runs over, the one named last changes fastest.
Arguments:
- tokens: bfloat16 [8, 1024, 2560], P('fsdp', 'context'), may hold values from -6 to 6
- norm_one: bfloat16 [2560], P(('fsdp', 'context')), may hold values from 0.099609375 to 1.8984375
- q_weight: bfloat16 [2560, 2560], P(('fsdp', 'context'), 'tensor'), may hold values from -0.125 to 0.125
- k_weight: bfloat16 [2560, 640], P(('fsdp', 'context'), 'tensor'), may hold values from -0.125 to 0.125
- v_weight: bfloat16 [2560, 640], P(('fsdp', 'context'), 'tensor'), may hold values from -0.125 to 0.125
- o_weight: bfloat16 [2560, 2560], P('tensor', ('fsdp', 'context')), may hold values from -0.5 to 0.5
- norm_two: bfloat16 [2560], P(('fsdp', 'context')), may hold values from 0.099609375 to 1.8984375
- gate_weight: bfloat16 [2560, 6912], P(('fsdp', 'context'), 'tensor'), may hold values from -0.125 to 0.125
- up_weight: bfloat16 [2560, 6912], P(('fsdp', 'context'), 'tensor'), may hold values from -0.125 to 0.125
- down_weight: bfloat16 [6912, 2560], P('tensor', ('fsdp', 'context')), may hold values from -0.15625 to 0.15625
- segment_ids: int32 [8, 1024], P('fsdp'), may hold values from 0 to 12, as said below
- parent_ids: int32 [8, 1024], P('fsdp'), may hold values from 0 to 4, as said below
- path_pos: int32 [8, 1024], P('fsdp'), may hold values from 0 to 607, as said below
- cotangent: bfloat16 [8, 1024, 2560], P('fsdp', 'context'), may hold values from -6 to 6
Outputs:
- layer_out: bfloat16 [8, 1024, 2560], P('fsdp', ('context', 'tensor'))
- tokens_grad: bfloat16 [8, 1024, 2560], P('fsdp', ('context', 'tensor'))
- norm_one_grad: float32 [2560], P(('fsdp', 'context'))
- q_grad: float32 [2560, 2560], P(('fsdp', 'context'), 'tensor')
- k_grad: float32 [2560, 640], P(('fsdp', 'context'), 'tensor')
- v_grad: float32 [2560, 640], P(('fsdp', 'context'), 'tensor')
- o_grad: float32 [2560, 2560], P('tensor', ('fsdp', 'context'))
- norm_two_grad: float32 [2560], P(('fsdp', 'context'))
- gate_grad: float32 [2560, 6912], P(('fsdp', 'context'), 'tensor')
- up_grad: float32 [2560, 6912], P(('fsdp', 'context'), 'tensor')
- down_grad: float32 [6912, 2560], P('tensor', ('fsdp', 'context'))
Inputs may be any that keep to these rules, and one draw needn't show every extreme that they name: `segment_ids`: in each tree, tokens 0 to 511 are segment 0, the trunk; the other tokens form 4 branches (segments 1 to 4, 64 tokens each) and 2 leaves per branch (32 tokens each, segments above 4); each segment is contiguous and each leaf comes after its branch. `parent_ids`: 0 for tokens of the trunk and of branches; for a leaf's tokens, the leaf's branch. `path_pos`: the trunk counts 0 upward; a branch continues from 512, a leaf from 576, each token one more than the one before it in its segment.
All inputs are finite; a program needn't handle non-finite values.
Results may differ from a plain program's by a relative error of at most 0.02.
Values may be sent and summed in bfloat16 or wider, within the bound.
A program may use at most 320 MiB of HBM per device.

v0:
```python
import jax
import jax.numpy as jnp
from jax import lax
from jax.sharding import PartitionSpec as P

HEADS = 32
KV_HEADS = 8
HEAD = 80
MICRO = 2


EPS = 1e-05
THETA = 10000.0
NEG = -1000000000.0


def scaled_norm(values, gain):
    return values * lax.rsqrt(jnp.mean(values * values, axis=-1, keepdims=True) + EPS) * gain


def swiglu(gate_in, up_in):
    return jax.nn.silu(gate_in) * up_in


def angle_tables(positions):
    half_width = HEAD // 2
    frequency = THETA ** (-(jnp.arange(half_width, dtype=jnp.float32) * 2.0 / HEAD))
    angles = positions.astype(jnp.float32)[:, None] * frequency[None, :]
    return (jnp.cos(angles), jnp.sin(angles))


def rotate(values, cosine, sine_part):
    half_width = values.shape[-1] // 2
    low_half = values[..., :half_width]
    high_half = values[..., half_width:]
    cos_rows = cosine[:, None, :]
    sin_rows = sine_part[:, None, :]
    return jnp.concatenate(
        [low_half * cos_rows - high_half * sin_rows, high_half * cos_rows + low_half * sin_rows],
        axis=-1,
    )


def outer_sum(left, right):
    return lax.dot_general(
        left, right, (((0,), (0,)), ((), ())), preferred_element_type=jnp.float32
    )


def back_product(left, right):
    return lax.dot_general(
        left, right, (((1,), (1,)), ((), ())), preferred_element_type=jnp.float32
    )


def block_scores(tree_q, keys_all, seg_tree, par_tree, pos_tree, row_start, block_rows):
    q_block = lax.dynamic_slice_in_dim(tree_q, row_start, block_rows, 0)
    seg_query = lax.dynamic_slice_in_dim(seg_tree, row_start, block_rows, 0)
    par_query = lax.dynamic_slice_in_dim(par_tree, row_start, block_rows, 0)
    pos_query = lax.dynamic_slice_in_dim(pos_tree, row_start, block_rows, 0)
    same_path = (
        (seg_tree[None, :] == seg_query[:, None])
        | (seg_tree[None, :] == par_query[:, None])
        | (seg_tree[None, :] == 0)
    )
    allowed = same_path & (pos_tree[None, :] <= pos_query[:, None])
    scores = jnp.einsum(
        "qhd,khd->hqk", q_block, keys_all, preferred_element_type=jnp.float32
    ) * HEAD ** (-0.5)
    return (q_block, jnp.where(allowed[None], scores, NEG))


def attend_forward(queries, keys_all, values_all, seg_trees, par_trees, pos_trees):
    tree_len = queries.shape[1]
    block_rows = min(tree_len, 512)
    block_count = tree_len // block_rows

    def one_tree(inputs):
        tree_q, tree_k, tree_v, seg_tree, par_tree, pos_tree = inputs

        def one_block(block_index):
            q_block, scores = block_scores(
                tree_q, tree_k, seg_tree, par_tree, pos_tree, block_index * block_rows, block_rows
            )
            row_max = jnp.max(scores, axis=-1, keepdims=True)
            exp_scores = jnp.exp(scores - row_max)
            row_total = jnp.sum(exp_scores, axis=-1, keepdims=True)
            probs_low = (exp_scores / row_total).astype(jnp.bfloat16)
            out_block = jnp.einsum(
                "hqk,khd->qhd", probs_low, tree_v, preferred_element_type=jnp.float32
            ).astype(jnp.bfloat16)
            return (out_block, row_max[..., 0] + jnp.log(row_total[..., 0]))

        out_blocks, log_sums = lax.map(one_block, jnp.arange(block_count))
        return (out_blocks.reshape(tree_q.shape), log_sums)

    return lax.map(one_tree, (queries, keys_all, values_all, seg_trees, par_trees, pos_trees))


def attend_backward(
    queries, keys_all, values_all, grad_out, log_sums, seg_trees, par_trees, pos_trees
):
    tree_len = queries.shape[1]
    block_rows = min(tree_len, 512)
    block_count = tree_len // block_rows
    score_scale = HEAD ** (-0.5)

    def one_tree(inputs):
        tree_q, tree_k, tree_v, tree_go, tree_lse, seg_tree, par_tree, pos_tree = inputs

        def one_block(grad_carry, block_index):
            key_grad, value_grad = grad_carry
            row_start = block_index * block_rows
            q_block, scores = block_scores(
                tree_q, tree_k, seg_tree, par_tree, pos_tree, row_start, block_rows
            )
            go_block = lax.dynamic_slice_in_dim(tree_go, row_start, block_rows, 0)
            probs_f32 = jnp.exp(scores - tree_lse[block_index][..., None])
            probs_low = probs_f32.astype(jnp.bfloat16)
            dprob = jnp.einsum("qhd,khd->hqk", go_block, tree_v, preferred_element_type=jnp.float32)
            row_delta = jnp.sum(probs_f32 * dprob, axis=-1, keepdims=True)
            dscore = (probs_f32 * (dprob - row_delta)).astype(jnp.bfloat16)
            query_grad = (
                jnp.einsum("hqk,khd->qhd", dscore, tree_k, preferred_element_type=jnp.float32)
                * score_scale
            )
            key_grad = (
                key_grad
                + jnp.einsum("hqk,qhd->khd", dscore, q_block, preferred_element_type=jnp.float32)
                * score_scale
            )
            value_grad = value_grad + jnp.einsum(
                "hqk,qhd->khd", probs_low, go_block, preferred_element_type=jnp.float32
            )
            return ((key_grad, value_grad), query_grad)

        zero_grad = jnp.zeros(tree_k.shape, jnp.float32)
        (key_grad, value_grad), query_grad = lax.scan(
            one_block, (zero_grad, zero_grad), jnp.arange(block_count)
        )
        return (query_grad.reshape(tree_q.shape), key_grad, value_grad)

    return lax.map(
        one_tree,
        (queries, keys_all, values_all, grad_out, log_sums, seg_trees, par_trees, pos_trees),
    )


def on_device(
    tokens,
    norm_one,
    q_weight,
    k_weight,
    v_weight,
    o_weight,
    norm_two,
    gate_weight,
    up_weight,
    down_weight,
    segment_ids,
    parent_ids,
    path_pos,
    cotangent,
):
    gathered = (
        lax.all_gather(q_weight, ("fsdp", "context"), axis=0, tiled=True),
        lax.all_gather(k_weight, ("fsdp", "context"), axis=0, tiled=True),
        lax.all_gather(v_weight, ("fsdp", "context"), axis=0, tiled=True),
        lax.all_gather(gate_weight, ("fsdp", "context"), axis=0, tiled=True),
        lax.all_gather(up_weight, ("fsdp", "context"), axis=0, tiled=True),
        lax.all_gather(norm_one, ("fsdp", "context"), axis=0, tiled=True),
        lax.all_gather(norm_two, ("fsdp", "context"), axis=0, tiled=True),
        lax.all_gather(o_weight, ("fsdp", "context"), axis=1, tiled=True),
        lax.all_gather(down_weight, ("fsdp", "context"), axis=1, tiled=True),
    )
    wq_full, wk_full, wv_full, wg_full, wu_full, gain_one, gain_two, wo_full, wd_full = gathered
    gain_f1 = gain_one.astype(jnp.float32)
    gain_f2 = gain_two.astype(jnp.float32)
    ctx_count = lax.axis_size("context")
    ctx_index = lax.axis_index("context")
    ten_count = lax.axis_size("tensor")
    ten_index = lax.axis_index("tensor")
    tree_count, local_len, model_width = tokens.shape
    tree_len = local_len * ctx_count
    share_len = local_len // ten_count
    q_width = wq_full.shape[1]
    kv_width = wk_full.shape[1]
    kv_local = kv_width // HEAD
    heads_tensor = q_width // HEAD
    heads_dev = heads_tensor // ctx_count
    group_size = HEADS // KV_HEADS
    batch_trees = tree_count // MICRO
    row_count = batch_trees * local_len

    def take_share(rows):
        shaped = rows.reshape(batch_trees, local_len, model_width)
        return lax.dynamic_slice_in_dim(shaped, ten_index * share_len, share_len, 1).reshape(
            batch_trees * share_len, model_width
        )

    def row_total(partial_rows):
        partial_value = partial_rows.reshape(batch_trees, local_len, model_width)
        total = lax.psum(partial_value, "tensor")
        return total.reshape(-1, model_width)

    grad_q = jnp.zeros(wq_full.shape, jnp.float32)
    grad_k = jnp.zeros(wk_full.shape, jnp.float32)
    grad_v = jnp.zeros(wv_full.shape, jnp.float32)
    grad_gate = jnp.zeros(wg_full.shape, jnp.float32)
    grad_up = jnp.zeros(wu_full.shape, jnp.float32)
    grad_out_proj = jnp.zeros(wo_full.shape, jnp.float32)
    grad_down = jnp.zeros(wd_full.shape, jnp.float32)
    grad_gain_one = jnp.zeros(gain_f1.shape, jnp.float32)
    grad_gain_two = jnp.zeros(gain_f2.shape, jnp.float32)
    outputs = []
    input_grads = []
    for micro_index in range(MICRO):
        first_tree = micro_index * batch_trees
        x_rows = (
            lax.slice_in_dim(tokens, first_tree, first_tree + batch_trees, axis=0)
            .reshape(row_count, model_width)
            .astype(jnp.float32)
        )
        seg_trees = lax.slice_in_dim(segment_ids, first_tree, first_tree + batch_trees, axis=0)
        par_trees = lax.slice_in_dim(parent_ids, first_tree, first_tree + batch_trees, axis=0)
        pos_trees = lax.slice_in_dim(path_pos, first_tree, first_tree + batch_trees, axis=0)
        pos_rows = lax.dynamic_slice_in_dim(pos_trees, ctx_index * local_len, local_len, 1).reshape(
            row_count
        )
        cosine, sine_part = angle_tables(pos_rows)
        normed_one, norm_one_back = jax.vjp(scaled_norm, x_rows, gain_f1)
        normed_low = normed_one.astype(jnp.bfloat16)
        q_rows = jnp.dot(normed_low, wq_full, preferred_element_type=jnp.float32)
        k_rows = jnp.dot(normed_low, wk_full, preferred_element_type=jnp.float32)
        v_rows = jnp.dot(normed_low, wv_full, preferred_element_type=jnp.float32)
        q_rot = rotate(q_rows.reshape(row_count, heads_tensor, HEAD), cosine, sine_part).astype(
            jnp.bfloat16
        )
        k_rot = rotate(k_rows.reshape(row_count, kv_local, HEAD), cosine, sine_part).astype(
            jnp.bfloat16
        )
        v_low = v_rows.astype(jnp.bfloat16)
        q_send = q_rot.reshape(batch_trees, local_len, q_width)
        k_wide = jnp.repeat(k_rot, group_size, axis=1).reshape(batch_trees, local_len, q_width)
        v_wide = jnp.repeat(v_low.reshape(row_count, kv_local, HEAD), group_size, axis=1).reshape(
            batch_trees, local_len, q_width
        )
        q_heads, k_heads, v_heads = (
            lax.all_to_all(q_send, "context", split_axis=2, concat_axis=1, tiled=True),
            lax.all_to_all(k_wide, "context", split_axis=2, concat_axis=1, tiled=True),
            lax.all_to_all(v_wide, "context", split_axis=2, concat_axis=1, tiled=True),
        )
        k_heads = k_heads.reshape(batch_trees, tree_len, heads_dev, HEAD)
        v_heads = v_heads.reshape(batch_trees, tree_len, heads_dev, HEAD)
        q_heads = q_heads.reshape(batch_trees, tree_len, heads_dev, HEAD)
        attended, log_sums = attend_forward(
            q_heads, k_heads, v_heads, seg_trees, par_trees, pos_trees
        )
        att_back = lax.all_to_all(
            attended.reshape(batch_trees, tree_len, heads_dev * HEAD),
            "context",
            split_axis=1,
            concat_axis=2,
            tiled=True,
        )
        att_rows = att_back.reshape(row_count, q_width)
        middle = x_rows + row_total(jnp.dot(att_rows, wo_full, preferred_element_type=jnp.float32))
        normed_two, norm_two_back = jax.vjp(scaled_norm, middle, gain_f2)
        normed_two_here = normed_two.astype(jnp.bfloat16)
        gate_rows = jnp.dot(normed_two_here, wg_full, preferred_element_type=jnp.float32)
        upward = jnp.dot(normed_two_here, wu_full, preferred_element_type=jnp.float32)
        mixed_rows, mix_back = jax.vjp(swiglu, gate_rows, upward)
        mixed_low = mixed_rows.astype(jnp.bfloat16)
        layer_here = (
            middle + row_total(jnp.dot(mixed_low, wd_full, preferred_element_type=jnp.float32))
        ).astype(jnp.bfloat16)
        layer_here = take_share(layer_here)
        outputs.append(layer_here.reshape(batch_trees, share_len, model_width))
        out_grad = (
            lax.slice_in_dim(cotangent, first_tree, first_tree + batch_trees, axis=0)
            .reshape(row_count, model_width)
            .astype(jnp.float32)
        )
        out_low = out_grad.astype(jnp.bfloat16)
        grad_down = grad_down + outer_sum(mixed_low, out_low)
        mixed_grad = back_product(out_low, wd_full)
        gate_grad_rows, up_grad_rows = mix_back(mixed_grad)
        gate_low = gate_grad_rows.astype(jnp.bfloat16)
        up_low = up_grad_rows.astype(jnp.bfloat16)
        grad_gate = grad_gate + outer_sum(normed_two_here, gate_low)
        grad_up = grad_up + outer_sum(normed_two_here, up_low)
        normed_two_grad = row_total(back_product(gate_low, wg_full) + back_product(up_low, wu_full))
        middle_part, gain_two_part = norm_two_back(normed_two_grad)
        grad_gain_two = grad_gain_two + gain_two_part
        middle_grad = out_grad + middle_part
        middle_here_low = middle_grad.astype(jnp.bfloat16)
        grad_out_proj = grad_out_proj + outer_sum(att_rows, middle_here_low)
        att_grad = (
            back_product(middle_here_low, wo_full)
            .astype(jnp.bfloat16)
            .reshape(batch_trees, local_len, q_width)
        )
        att_grad_heads = lax.all_to_all(
            att_grad, "context", split_axis=2, concat_axis=1, tiled=True
        ).reshape(batch_trees, tree_len, heads_dev, HEAD)
        q_grad_heads, k_grad_heads, v_grad_heads = attend_backward(
            q_heads, k_heads, v_heads, att_grad_heads, log_sums, seg_trees, par_trees, pos_trees
        )
        q_grad_tokens = lax.all_to_all(
            q_grad_heads.astype(jnp.bfloat16).reshape(batch_trees, tree_len, heads_dev * HEAD),
            "context",
            split_axis=1,
            concat_axis=2,
            tiled=True,
        )
        k_back, v_back = (
            lax.all_to_all(
                k_grad_heads.reshape(batch_trees, tree_len, heads_dev * HEAD).astype(jnp.bfloat16),
                "context",
                split_axis=1,
                concat_axis=2,
                tiled=True,
            ).astype(jnp.float32),
            lax.all_to_all(
                v_grad_heads.reshape(batch_trees, tree_len, heads_dev * HEAD).astype(jnp.bfloat16),
                "context",
                split_axis=1,
                concat_axis=2,
                tiled=True,
            ).astype(jnp.float32),
        )
        k_grad_rows = jnp.sum(k_back.reshape(row_count, kv_local, group_size, HEAD), axis=2)
        v_grad_rows = jnp.sum(v_back.reshape(row_count, kv_local, group_size, HEAD), axis=2)
        k_grad_low = lax.optimization_barrier(k_grad_rows.astype(jnp.bfloat16)).astype(jnp.float32)
        k_pre = (
            rotate(k_grad_low, cosine, -sine_part).astype(jnp.bfloat16).reshape(row_count, kv_width)
        )
        q_pre = (
            rotate(
                q_grad_tokens.astype(jnp.float32).reshape(row_count, heads_tensor, HEAD),
                cosine,
                -sine_part,
            )
            .astype(jnp.bfloat16)
            .reshape(row_count, q_width)
        )
        v_pre = v_grad_rows.reshape(row_count, kv_width).astype(jnp.bfloat16)
        grad_q = grad_q + outer_sum(normed_low, q_pre)
        grad_k = grad_k + outer_sum(normed_low, k_pre)
        grad_v = grad_v + outer_sum(normed_low, v_pre)
        normed_one_grad = row_total(
            back_product(q_pre, wq_full)
            + back_product(k_pre, wk_full)
            + back_product(v_pre, wv_full)
        )
        x_part, gain_one_part = norm_one_back(normed_one_grad)
        grad_gain_one = grad_gain_one + gain_one_part
        input_here = (middle_grad + x_part).astype(jnp.bfloat16)
        input_here = take_share(input_here)
        input_grads.append(input_here.reshape(batch_trees, share_len, model_width))
    summed = (
        lax.psum_scatter(
            grad_q.astype(jnp.bfloat16), ("fsdp", "context"), scatter_dimension=0, tiled=True
        ).astype(jnp.float32),
        lax.psum_scatter(
            grad_k.astype(jnp.bfloat16), ("fsdp", "context"), scatter_dimension=0, tiled=True
        ).astype(jnp.float32),
        lax.psum_scatter(
            grad_v.astype(jnp.bfloat16), ("fsdp", "context"), scatter_dimension=0, tiled=True
        ).astype(jnp.float32),
        lax.psum_scatter(
            grad_gate.astype(jnp.bfloat16), ("fsdp", "context"), scatter_dimension=0, tiled=True
        ).astype(jnp.float32),
        lax.psum_scatter(
            grad_up.astype(jnp.bfloat16), ("fsdp", "context"), scatter_dimension=0, tiled=True
        ).astype(jnp.float32),
        lax.psum_scatter(
            grad_gain_one.astype(jnp.bfloat16), ("fsdp", "context"), scatter_dimension=0, tiled=True
        ).astype(jnp.float32),
        lax.psum_scatter(
            grad_gain_two.astype(jnp.bfloat16), ("fsdp", "context"), scatter_dimension=0, tiled=True
        ).astype(jnp.float32),
        lax.psum_scatter(
            grad_out_proj.astype(jnp.bfloat16), ("fsdp", "context"), scatter_dimension=1, tiled=True
        ).astype(jnp.float32),
        lax.psum_scatter(
            grad_down.astype(jnp.bfloat16), ("fsdp", "context"), scatter_dimension=1, tiled=True
        ).astype(jnp.float32),
    )
    gain_one_grad = summed[5]
    gain_two_grad = summed[6]
    layer_out = jnp.concatenate(outputs, axis=0)
    tokens_grad = jnp.concatenate(input_grads, axis=0)
    return (
        layer_out,
        tokens_grad,
        gain_one_grad,
        summed[0],
        summed[1],
        summed[2],
        summed[7],
        gain_two_grad,
        summed[3],
        summed[4],
        summed[8],
    )


def solution(mesh):
    return jax.shard_map(
        on_device,
        mesh=mesh,
        in_specs=(
            P("fsdp", "context", None),
            P(("fsdp", "context")),
            P(("fsdp", "context"), "tensor"),
            P(("fsdp", "context"), "tensor"),
            P(("fsdp", "context"), "tensor"),
            P("tensor", ("fsdp", "context")),
            P(("fsdp", "context")),
            P(("fsdp", "context"), "tensor"),
            P(("fsdp", "context"), "tensor"),
            P("tensor", ("fsdp", "context")),
            P("fsdp", None),
            P("fsdp", None),
            P("fsdp", None),
            P("fsdp", "context", None),
        ),
        out_specs=(
            P("fsdp", ("context", "tensor"), None),
            P("fsdp", ("context", "tensor"), None),
            P(("fsdp", "context")),
            P(("fsdp", "context"), "tensor"),
            P(("fsdp", "context"), "tensor"),
            P(("fsdp", "context"), "tensor"),
            P("tensor", ("fsdp", "context")),
            P(("fsdp", "context")),
            P(("fsdp", "context"), "tensor"),
            P(("fsdp", "context"), "tensor"),
            P("tensor", ("fsdp", "context")),
        ),
        check_vma=False,
    )
```

profile of v0, /device:TPU:0, one launch (start us, length us, event | category | flops | bytes accessed | tf_op | source)
XLA Modules:
  0.0 2783.7 jit_solution(11389675260428864159)
XLA Ops:
  11.7 26.4 all-reduce.8
  38.1 20.5 all-gather
  79.3 25.5 all-gather.1
  218.8 20.2 while.94
  268.3 19.2 while.95
  333.6 356.1 %all-reduce.17.cloned.1.call-done = (f32[1,512,2560]{2,1,0:T(8,128)}, f32[1,512,2560]{2,1,0:T(8,128)}) async-done(((f32[1,512,2560]{2,1,0:T(8,128)}, f32[1,512,2560]{2,1,0:T(8,128)}), (f32[1,512,2560]{2,1,0:T(8,128)}, f32[1,512,2560]{2,1,0:T(8,128)})) %all-reduce.17.cloned.1.call-update) | async-done | bytes 10485776 | tf_op jit(solution)/shard_map/psum | solution.py:203
  703.6 44.4 %all-gather.12.cloned.1.call-done = bf16[2560,1728]{1,0:T(8,128)(2,1)} async-done(((bf16[320,1728]{1,0:T(8,128)(2,1)}), bf16[2560,1728]{1,0:T(8,128)(2,1)}) %all-gather.12.cloned.1.call-update) | async-done | bytes 8847376 | tf_op jit(solution)/shard_map/all_gather | solution.py:169
  748.0 11.0 fusion.227
  759.0 48.3 %all-gather.14.cloned.1.call-done = bf16[2560,1728]{1,0:T(8,128)(2,1)} async-done(((bf16[320,1728]{1,0:T(8,128)(2,1)}), bf16[2560,1728]{1,0:T(8,128)(2,1)}) %all-gather.14.cloned.1.call-update) | async-done | bytes 8847376 | tf_op jit(solution)/shard_map/all_gather | solution.py:170
  807.3 11.1 fusion.228
  834.4 32.2 %all-gather.16.cloned.1.call-done = bf16[1728,2560]{0,1:T(8,128)(2,1)} async-done(((bf16[1728,320]{0,1:T(8,128)(2,1)}), bf16[1728,2560]{0,1:T(8,128)(2,1)}) %all-gather.16.cloned.1.call-update) | async-done | bytes 8847376 | tf_op jit(solution)/shard_map/all_gather | solution.py:174
  866.7 14.0 multiply_convert_fusion.5
  880.7 12.0 fusion.233
  892.7 15.2 multiply_convert_fusion.4
  907.9 11.6 fusion.236
  919.5 11.5 add_bitcast_fusion.1
  939.7 358.6 %all-reduce.15.cloned.1.call-done = (f32[1,512,2560]{2,1,0:T(8,128)}, f32[1,512,2560]{2,1,0:T(8,128)}) async-done(((f32[1,512,2560]{2,1,0:T(8,128)}, f32[1,512,2560]{2,1,0:T(8,128)}), (f32[1,512,2560]{2,1,0:T(8,128)}, f32[1,512,2560]{2,1,0:T(8,128)})) %all-reduce.15.cloned.1.call-update) | async-done | bytes 10485776 | tf_op jit(solution)/shard_map/psum | solution.py:203
  1369.0 65.4 %while.96 = (s32[]{:T(128)}, f32[1024,4,80]{0,2,1:T(8,128)}, f32[1024,4,80]{0,2,1:T(8,128)}, bf16[2,512,4,80]{1,3,2,0:T(8,128)(2,1)}, s32[2]{0:T(128)S(1)}, /*in...) while((s32[]{:T(128)}, f32[1024,4,80]{0,2,1:T(8,128)}, ...), condition=%wide.region_20.21_spmd.clone, body=%wide.region_18.20_spmd.clone.sunk | while | flops 1714125824 | bytes 135619488 | solution.py:138
  1462.9 63.5 %while.97 = (s32[]{:T(128)}, f32[1024,4,80]{0,2,1:T(8,128)S(1)}, f32[1024,4,80]{0,2,1:T(8,128)}, bf16[2,512,4,80]{1,3,2,0:T(8,128)(2,1)}, s32[2]{0:T(128)S(1)}, ...) while((s32[]{:T(128)}, f32[1024,4,80]{0,2,1:T(8,128)S(1)}, ...), condition=%wide.region_29.30_spmd.clone, body=%wide.region_27.29_spmd.clone.sunk | while | flops 1714125824 | bytes 135619488 | solution.py:138
  1542.7 13.7 fusion.240
  1622.9 16.4 add_convert_fusion.1
  1639.5 13.7 fusion.239
  1653.2 12.2 add_convert_fusion.2
  1666.9 11.2 fusion.130
  1678.1 16.5 add_convert_fusion
  1785.0 12.3 fusion.229
  1837.6 14.1 reduce-scatter.16.cloned.1.call-done
  1854.5 76.0 %reduce-scatter.20.cloned.1.call-done = bf16[1728,320]{0,1:T(8,128)(2,1)} async-done(((bf16[1728,2560]{0,1:T(8,128)(2,1)}), bf16[1728,320]{0,1:T(8,128)(2,1)}) %reduce-scatter.20.cloned.1.call-update) | async-done | bytes 1105936 | tf_op jit(solution)/shard_map/reduce_scatter | solution.py:386
  1933.3 47.4 %reduce-scatter.14.cloned.1.call-done = bf16[640,320]{0,1:T(8,128)(2,1)} async-done(((bf16[640,2560]{0,1:T(8,128)(2,1)}), bf16[640,320]{0,1:T(8,128)(2,1)}) %reduce-scatter.14.cloned.1.call-update) | async-done | bytes 409616 | tf_op jit(solution)/shard_map/reduce_scatter | solution.py:383
  1982.7 48.1 %reduce-scatter.12.cloned.1.call-done = bf16[320,640]{1,0:T(8,128)(2,1)} async-done(((bf16[2560,640]{1,0:T(8,128)(2,1)}), bf16[320,640]{1,0:T(8,128)(2,1)}) %reduce-scatter.12.cloned.1.call-update) | async-done | bytes 409616 | tf_op jit(solution)/shard_map/reduce_scatter | solution.py:362
  2032.7 698.5 %all-reduce.13.cloned.1.call-done = (f32[512,2560]{1,0:T(8,128)}, f32[512,2560]{1,0:T(8,128)}, f32[512,2560]{1,0:T(8,128)}, f32[512,2560]{1,0:T(8,128)}) async-done(((f32[512,2560]{1,0:T(8,128)}, f32[512,2560]{1,0:T(8,128)}, f32[512,2560]{1,0:T(8,128)}, f32[512,2560]{1,0:T(8,128)}), (f32[512,2560]{1,0:T(8,128)}, f32[512,2560]{1,0:T(8,128)}, f32[512,2560]{1,0:T(8,128)}, ...) | async-done | bytes 20971536 | tf_op jit(solution)/shard_map/psum | solution.py:203
  2740.6 24.0 all-reduce.7
  (657 shorter events, 750.0 us)
Async XLA Ops:
  7.2 158.7 %all-gather.8.cloned.1.call-start = ((), (), s32[]{:S(2)}) async-start(), calls=%async_computation.23 | async-start | bytes 3686400 | tf_op jit(solution)/shard_map/all_gather | solution.py:166
  74.3 46.3 %all-to-all-start.1 = ((bf16[2,2,81920]{2,1,0:T(2,128)(2,1)}), bf16[2,2,81920]{2,1,0:T(2,128)(2,1)}, u32[]{:S(2)}, u32[]{:S(2)}) async-start(bf16[2,2,81920]{2,1,0:T(2,128)(2,1)} %reshape.1309), calls=%async_computation.1 | async-start | bytes 1310720 | tf_op jit(solution)/shard_map/all_to_all | solution.py:250
  78.5 241.8 %all-gather.10.cloned.1.call-start = ((), (), s32[]{:S(2)}) async-start(), calls=%async_computation.24 | async-start | bytes 3686400 | tf_op jit(solution)/shard_map/all_gather | solution.py:173
  120.5 14.8 all-to-all-start.2
  135.3 13.6 all-to-all-start.5
  148.9 14.0 all-to-all-start.6
  190.9 14.9 all-to-all-start
  205.7 52.7 %all-to-all-start.4 = ((bf16[2,2,81920]{2,1,0:T(2,128)(2,1)}), bf16[2,2,81920]{2,1,0:T(2,128)(2,1)}, u32[]{:S(2)}, u32[]{:S(2)}) async-start(bf16[2,2,81920]{2,1,0:T(2,128)(2,1)} %reshape.1299), calls=%async_computation.4 | async-start | bytes 1310720 | tf_op jit(solution)/shard_map/all_to_all | solution.py:249
  258.4 45.5 %all-to-all-start.3 = ((bf16[2,2,81920]{2,1,0:T(2,128)(2,1)}), bf16[2,2,81920]{2,1,0:T(2,128)(2,1)}, u32[]{:S(2)}, u32[]{:S(2)}) async-start(bf16[2,2,81920]{2,1,0:T(2,128)(2,1)} %reshape.1313), calls=%async_computation.3 | async-start | bytes 1310720 | tf_op jit(solution)/shard_map/all_to_all | solution.py:259
  303.9 13.1 all-to-all-start.7
  308.2 381.5 %all-reduce.17.cloned.1.call-start = ((), (), s32[]{:S(2)}) async-start(), calls=%async_computation.37 | async-start | bytes 20971520 | tf_op jit(solution)/shard_map/psum | solution.py:203
  331.7 416.2 %all-gather.12.cloned.1.call-start = ((), (), s32[]{:S(2)}) async-start(), calls=%async_computation.25 | async-start | bytes 10321920 | tf_op jit(solution)/shard_map/all_gather | solution.py:169
  332.3 475.0 %all-gather.14.cloned.1.call-start = ((), (), s32[]{:S(2)}) async-start(), calls=%async_computation.26 | async-start | bytes 10321920 | tf_op jit(solution)/shard_map/all_gather | solution.py:170
  332.9 533.8 %all-gather.16.cloned.1.call-start = ((), (), s32[]{:S(2)}) async-start(), calls=%async_computation.27 | async-start | bytes 10321920 | tf_op jit(solution)/shard_map/all_gather | solution.py:174
  333.5 964.9 %all-reduce.15.cloned.1.call-start = ((), (), s32[]{:S(2)}) async-start(), calls=%async_computation.36 | async-start | bytes 20971520 | tf_op jit(solution)/shard_map/psum | solution.py:203
  333.5 974.1 %copy-start.58 = (f32[2560]{0:T(1024)}, f32[2560]{0:T(1024)S(1)}, u32[]{:S(2)}) copy-start(f32[2560]{0:T(1024)S(1)} %convert_element_type.529) | copy-start | bytes 30724
  1334.4 20.9 all-to-all-start.8
  1355.3 93.7 %all-to-all-start.12 = ((bf16[2,2,81920]{2,1,0:T(2,128)(2,1)}), bf16[2,2,81920]{2,1,0:T(2,128)(2,1)}, u32[]{:S(2)}, u32[]{:S(2)}) async-start(bf16[2,2,81920]{2,1,0:T(2,128)(2,1)} %reshape.1315), calls=%async_computation.12 | async-start | bytes 1310720 | tf_op jit(solution)/shard_map/all_to_all | solution.py:303
  1449.0 90.2 %all-to-all-start.11 = ((bf16[2,2,81920]{2,1,0:T(2,128)(2,1)}), bf16[2,2,81920]{2,1,0:T(2,128)(2,1)}, u32[]{:S(2)}, u32[]{:S(2)}) async-start(bf16[2,2,81920]{2,1,0:T(2,128)(2,1)} %reshape.1329), calls=%async_computation.11 | async-start | bytes 1310720 | tf_op jit(solution)/shard_map/all_to_all | solution.py:324
  1539.2 45.6 %all-to-all-start.15 = ((bf16[2,2,81920]{2,1,0:T(2,128)(2,1)}), bf16[2,2,81920]{2,1,0:T(2,128)(2,1)S(1)}, u32[]{:S(2)}, u32[]{:S(2)}) async-start(bf16[2,2,81920]{2,1,0:T(2,128)(2,1)} %reshape.1321), calls=%async_computation.15 | async-start | bytes 1310720 | tf_op jit(solution)/shard_map/all_to_all | solution.py:324
  1584.8 13.8 all-to-all-start.10
  1598.6 12.8 all-to-all-start.14
  1602.1 229.0 %reduce-scatter.24.cloned.1.call-start = ((), (), s32[]{:S(2)}) async-start(), calls=%async_computation.34 | async-start | bytes 1474560
  1606.4 226.5 %reduce-scatter.22.cloned.1.call-start = ((), (), s32[]{:S(2)}) async-start(), calls=%async_computation.33 | async-start | bytes 1474560
  1622.8 211.8 %reduce-scatter.18.cloned.1.call-start = ((), (), s32[]{:S(2)}) async-start(), calls=%async_computation.31 | async-start | bytes 10321920 | tf_op jit(solution)/shard_map/reduce_scatter | solution.py:374
  1639.3 212.4 %reduce-scatter.16.cloned.1.call-start = ((), (), s32[]{:S(2)}) async-start(), calls=%async_computation.30 | async-start | bytes 10321920 | tf_op jit(solution)/shard_map/reduce_scatter | solution.py:371
  1665.4 265.1 %reduce-scatter.20.cloned.1.call-start = ((), (), s32[]{:S(2)}) async-start(), calls=%async_computation.32 | async-start | bytes 10321920 | tf_op jit(solution)/shard_map/reduce_scatter | solution.py:386
  1694.7 286.1 %reduce-scatter.14.cloned.1.call-start = ((), (), s32[]{:S(2)}) async-start(), calls=%async_computation.29 | async-start | bytes 3686400 | tf_op jit(solution)/shard_map/reduce_scatter | solution.py:383
  1727.4 19.7 all-to-all-start.9
  1747.0 20.0 all-to-all-start.13
  1751.3 279.4 %reduce-scatter.12.cloned.1.call-start = ((), (), s32[]{:S(2)}) async-start(), calls=%async_computation.28 | async-start | bytes 3686400 | tf_op jit(solution)/shard_map/reduce_scatter | solution.py:362
  1784.8 946.5 %all-reduce.13.cloned.1.call-start = ((), (), s32[]{:S(2)}) async-start(), calls=%async_computation.35 | async-start | bytes 41943040 | tf_op jit(solution)/shard_map/psum | solution.py:203
  (122 other events, 3679.8 us)
Sparse Core Ops, SparseCore 0:
  9.9 37.1 all-gather.7
  81.2 35.5 all-gather.9
  331.9 357.7 all-reduce.16
  691.4 56.5 all-gather.11
  749.7 57.5 all-gather.13
  809.0 57.5 all-gather.15
  939.8 358.4 all-reduce.14
  1606.5 36.8 reduce-scatter.23
  1646.7 37.1 reduce-scatter.21
  1687.4 87.2 reduce-scatter.17
  1778.3 73.3 reduce-scatter.15
  1855.2 75.3 reduce-scatter.19
  1933.9 46.7 reduce-scatter.13
  1984.0 46.7 reduce-scatter.11
  2033.5 697.6 all-reduce.12
where the time goes:
time: 2800 us; the launch traced here: 2780 us
  waiting for transfers between devices  1750 us (62%)
  matrix products  428 us (15%)
  other arithmetic  216 us (8%)
  local copies, waits for them, and re-layouts  191 us (7%)
  blocking collectives  96.4 us (3%)
  starting transfers between devices  68.6 us (2%)
    psum x3, waiting for transfers between devices, row_total(): total = lax.psum(partial_value, 'tensor')  1410 us
    dot_general x14, matrix products, outer_sum(): lax.dot_general(left, right, (((0,), (0,)), ((), ())), preferred_element_...  121 us
    dot_general x14, matrix products, back_product(): lax.dot_general(left, right, (((1,), (1,)), ((), ())), preferred_element_...  97.1 us
    unnamed x24, other arithmetic  93.6 us
    unnamed x272, local copies, waits for them, and re-layouts  89.7 us
    reduce_scatter x1, waiting for transfers between devices, on_device(): lax.psum_scatter(grad_down.astype(jnp.bfloat16), ('fsdp', 'context'), sca...  76 us
  transfers between devices with their start and end apart: 31, of which 16 were waited for; matrix products, arithmetic and copies ran while one was open for 25% of the time, Pallas kernels for 0%

commit v1 on v0

v1 whole, which is shorter than its diff:
```python
import functools

import jax
import jax.numpy as jnp
import numpy as np
from jax import lax
from jax.experimental import pallas as pl
from jax.experimental.pallas import tpu as pltpu
from jax.sharding import PartitionSpec as P

HEADS = 32
KV_HEADS = 8
HEAD = 80
HALF = HEAD // 2
LANES = 128
MICRO = 2
EPS = 1e-05
THETA = 10000.0
NEG = -1000000000.0
TRUNK = 512
WEIGHT_AXES = ("fsdp", "context")
BF16 = jnp.bfloat16
F32 = jnp.float32


def round_up(value, unit):
    return (value + unit - 1) // unit * unit


def mm(left, right):
    return lax.dot_general(left, right, (((1,), (0,)), ((), ())), preferred_element_type=F32)


def mm_nt(left, right):
    return lax.dot_general(left, right, (((1,), (1,)), ((), ())), preferred_element_type=F32)


def mm_tn(left, right):
    return lax.dot_general(left, right, (((0,), (0,)), ((), ())), preferred_element_type=F32)


def rotated(values, cos_table, sin_table):
    lane = lax.broadcasted_iota(jnp.int32, values.shape, 1)
    swapped = jnp.where(
        lane < HALF, pltpu.roll(values, LANES - HALF, 1), pltpu.roll(values, HALF, 1)
    )
    return values * cos_table + swapped * sin_table


def window_of(head):
    start = head * HEAD
    base = start // LANES * LANES
    return base, start - base


def split_kernel(q_heads, kv_heads, x_ref, cos_ref, sin_ref, q_ref, kv_ref):
    cos_table = cos_ref[...]
    sin_table = sin_ref[...]
    for head in range(q_heads + 2 * kv_heads):
        base, shift = window_of(head)
        window = x_ref[:, base : base + 2 * LANES]
        if shift:
            window = pltpu.roll(window, 2 * LANES - shift, 1)
        values = window[:, :LANES]
        if head < q_heads + kv_heads:
            result = rotated(values, cos_table, sin_table)
        else:
            lane = lax.broadcasted_iota(jnp.int32, values.shape, 1)
            result = jnp.where(lane < HEAD, values, 0.0)
        result = result.astype(BF16)
        if head < q_heads:
            q_ref[:, head * LANES : (head + 1) * LANES] = result
        else:
            at = (head - q_heads) * LANES
            kv_ref[:, at : at + LANES] = result


def split_heads(packed, cos_table, sin_table, q_heads, kv_heads, rows):
    total, width = packed.shape
    q_wide = q_heads * LANES
    kv_wide = 2 * kv_heads * LANES
    return pl.pallas_call(
        functools.partial(split_kernel, q_heads, kv_heads),
        grid=(total // rows,),
        in_specs=[
            pl.BlockSpec((rows, width), lambda b: (b, 0)),
            pl.BlockSpec((rows, LANES), lambda b: (b, 0)),
            pl.BlockSpec((rows, LANES), lambda b: (b, 0)),
        ],
        out_specs=[
            pl.BlockSpec((rows, q_wide), lambda b: (b, 0)),
            pl.BlockSpec((rows, kv_wide), lambda b: (b, 0)),
        ],
        out_shape=[
            jax.ShapeDtypeStruct((total, q_wide), BF16),
            jax.ShapeDtypeStruct((total, kv_wide), BF16),
        ],
        cost_estimate=pl.CostEstimate(
            flops=10 * total * width, bytes_accessed=7 * total * width, transcendentals=0
        ),
        name="split_heads",
    )(packed, cos_table, sin_table)


def pack_kernel(q_heads, kv_heads, dq_ref, dkv_ref, cos_ref, sin_ref, out_ref, sum_ref):
    cos_table = cos_ref[...]
    sin_table = -sin_ref[...]
    sum_ref[...] = jnp.zeros_like(sum_ref)
    for head in range(q_heads + 2 * kv_heads):
        base, shift = window_of(head)
        if head < q_heads:
            values = dq_ref[:, head * LANES : (head + 1) * LANES].astype(F32)
        else:
            at = (head - q_heads) * LANES
            values = dkv_ref[:, at : at + LANES].astype(BF16).astype(F32)
        if head < q_heads + kv_heads:
            values = rotated(values, cos_table, sin_table)
        wide = jnp.concatenate([values, jnp.zeros_like(values)], axis=1)
        if shift:
            wide = pltpu.roll(wide, shift, 1)
        sum_ref[:, base : base + 2 * LANES] += wide
    out_ref[...] = sum_ref[...].astype(BF16)


def pack_heads(dq_wide, dkv, cos_table, sin_table, q_heads, kv_heads, width, rows):
    total = dq_wide.shape[0]
    return pl.pallas_call(
        functools.partial(pack_kernel, q_heads, kv_heads),
        grid=(total // rows,),
        in_specs=[
            pl.BlockSpec((rows, dq_wide.shape[1]), lambda b: (b, 0)),
            pl.BlockSpec((rows, dkv.shape[1]), lambda b: (b, 0)),
            pl.BlockSpec((rows, LANES), lambda b: (b, 0)),
            pl.BlockSpec((rows, LANES), lambda b: (b, 0)),
        ],
        out_specs=pl.BlockSpec((rows, width), lambda b: (b, 0)),
        out_shape=jax.ShapeDtypeStruct((total, width), BF16),
        scratch_shapes=[pltpu.VMEM((rows, width), F32)],
        cost_estimate=pl.CostEstimate(
            flops=10 * total * width, bytes_accessed=7 * total * width, transcendentals=0
        ),
        name="pack_heads",
    )(dq_wide, dkv, cos_table, sin_table)


def fill_bias(seg_q, par_q, pos_q, seg_k, pos_k, bias_ref):
    same = (seg_k == seg_q) | (seg_k == par_q) | (seg_k == 0)
    bias_ref[...] = jnp.where(same & (pos_k <= pos_q), 0.0, NEG)


def probabilities(q_block, keys, bias):
    scores = mm_nt(q_block, keys) * HEAD ** (-0.5) + bias
    top = jnp.max(scores, axis=1, keepdims=True)
    raised = jnp.exp(scores - top)
    return raised * (1.0 / jnp.sum(raised, axis=1, keepdims=True))


def forward_kernel(
    rows, tree_len, block,
    ctx_ref, q_ref, k_ref, v_ref, seg_q, par_q, pos_q, seg_k, pos_k, out_ref, bias_ref,
):
    @pl.when(pl.program_id(1) == 0)
    def _():
        fill_bias(seg_q[0], par_q[0], pos_q[0], seg_k[0], pos_k[0], bias_ref)

    in_trunk = (ctx_ref[0] + 1) * rows <= TRUNK

    def run(keys):
        @pl.loop(0, rows // block)
        def _(step):
            at = pl.ds(pl.multiple_of(step * block, block), block)
            probs = probabilities(q_ref[at, :], k_ref[0, :keys, :], bias_ref[at, :keys])
            out_ref[at, :] = mm(probs.astype(BF16), v_ref[0, :keys, :]).astype(BF16)

    pl.when(in_trunk)(lambda: run(min(TRUNK, tree_len)))
    pl.when(jnp.logical_not(in_trunk))(lambda: run(tree_len))


def backward_kernel(
    rows, tree_len, block, group,
    ctx_ref, q_ref, k_ref, v_ref, do_ref, seg_q, par_q, pos_q, seg_k, pos_k,
    dq_ref, dk_ref, dv_ref, bias_ref,
):
    head = pl.program_id(1)

    @pl.when(head == 0)
    def _():
        fill_bias(seg_q[0], par_q[0], pos_q[0], seg_k[0], pos_k[0], bias_ref)

    @pl.when(lax.rem(head, group) == 0)
    def _():
        dk_ref[...] = jnp.zeros_like(dk_ref)
        dv_ref[...] = jnp.zeros_like(dv_ref)

    in_trunk = (ctx_ref[0] + 1) * rows <= TRUNK
    scale = HEAD ** (-0.5)

    def run(keys):
        @pl.loop(0, rows // block)
        def _(step):
            at = pl.ds(pl.multiple_of(step * block, block), block)
            q_block = q_ref[at, :]
            do_block = do_ref[at, :]
            k_all = k_ref[0, :keys, :]
            probs = probabilities(q_block, k_all, bias_ref[at, :keys])
            dprobs = mm_nt(do_block, v_ref[0, :keys, :])
            delta = jnp.sum(probs * dprobs, axis=1, keepdims=True)
            dscores = (probs * (dprobs - delta)).astype(BF16)
            dq_ref[at, :] = (mm(dscores, k_all) * scale).astype(BF16)
            dk_ref[0, :keys, :] += mm_tn(dscores, q_block) * scale
            dv_ref[0, :keys, :] += mm_tn(probs.astype(BF16), do_block)

    pl.when(in_trunk)(lambda: run(min(TRUNK, tree_len)))
    pl.when(jnp.logical_not(in_trunk))(lambda: run(tree_len))


def attention_specs(rows, tree_len, group, kv_heads):
    return [
        pl.BlockSpec((rows, LANES), lambda b, h, c: (b, h)),
        pl.BlockSpec((1, tree_len, LANES), lambda b, h, c: (b, 0, h // group)),
        pl.BlockSpec((1, tree_len, LANES), lambda b, h, c: (b, 0, kv_heads + h // group)),
    ], [
        pl.BlockSpec((1, rows, 1), lambda b, h, c: (b, 0, 0)),
        pl.BlockSpec((1, rows, 1), lambda b, h, c: (b, 0, 0)),
        pl.BlockSpec((1, rows, 1), lambda b, h, c: (b, 0, 0)),
        pl.BlockSpec((1, 1, tree_len), lambda b, h, c: (b, 0, 0)),
        pl.BlockSpec((1, 1, tree_len), lambda b, h, c: (b, 0, 0)),
    ]


def attend_forward(ctx, q_wide, kv_full, ids, q_heads, kv_heads, rows):
    trees, tree_len, _ = kv_full.shape
    group = q_heads // kv_heads
    first, last = attention_specs(rows, tree_len, group, kv_heads)
    block = min(rows, 256)
    work = trees * q_heads * rows * tree_len
    return pl.pallas_call(
        functools.partial(forward_kernel, rows, tree_len, block),
        grid_spec=pltpu.PrefetchScalarGridSpec(
            num_scalar_prefetch=1,
            grid=(trees, q_heads),
            in_specs=first + last,
            out_specs=pl.BlockSpec((rows, LANES), lambda b, h, c: (b, h)),
            scratch_shapes=[pltpu.VMEM((rows, tree_len), F32)],
        ),
        out_shape=jax.ShapeDtypeStruct(q_wide.shape, BF16),
        cost_estimate=pl.CostEstimate(
            flops=4 * LANES * work, bytes_accessed=8 * q_wide.size, transcendentals=work
        ),
        name="attend_forward",
    )(ctx, q_wide, kv_full, kv_full, *ids)


def attend_backward(ctx, q_wide, kv_full, do_wide, ids, q_heads, kv_heads, rows):
    trees, tree_len, _ = kv_full.shape
    group = q_heads // kv_heads
    first, last = attention_specs(rows, tree_len, group, kv_heads)
    block = min(rows, 256)
    work = trees * q_heads * rows * tree_len
    grad_spec = pl.BlockSpec((1, tree_len, LANES), lambda b, h, c: (b, 0, h // group))
    grad_shape = jax.ShapeDtypeStruct((trees, tree_len, kv_heads * LANES), F32)
    return pl.pallas_call(
        functools.partial(backward_kernel, rows, tree_len, block, group),
        grid_spec=pltpu.PrefetchScalarGridSpec(
            num_scalar_prefetch=1,
            grid=(trees, q_heads),
            in_specs=first + [first[0]] + last,
            out_specs=[first[0], grad_spec, grad_spec],
            scratch_shapes=[pltpu.VMEM((rows, tree_len), F32)],
        ),
        out_shape=[jax.ShapeDtypeStruct(q_wide.shape, BF16), grad_shape, grad_shape],
        cost_estimate=pl.CostEstimate(
            flops=10 * LANES * work, bytes_accessed=12 * q_wide.size, transcendentals=work
        ),
        name="attend_backward",
    )(ctx, q_wide, kv_full, kv_full, do_wide, *ids)


def piece(values, index, size):
    return lax.dynamic_slice_in_dim(values, index * size, size, 1)


def line_reduce_scatter(partial_rows, size, axis):
    count = lax.axis_size(axis)
    here = lax.axis_index(axis)
    from_left = None
    from_right = None
    for step in range(1, count):
        index = jnp.clip(count - step + here, 0, count - 1)
        value = piece(partial_rows, index, size)
        if from_left is not None:
            value = value + from_left.astype(F32)
        pairs = [(i, i + 1) for i in range(step)]
        next_left = lax.ppermute(value.astype(BF16), axis, pairs)
        index = jnp.clip(here - (count - step), 0, count - 1)
        value = piece(partial_rows, index, size)
        if from_right is not None:
            value = value + from_right.astype(F32)
        pairs = [(count - 1 - i, count - 2 - i) for i in range(step)]
        next_right = lax.ppermute(value.astype(BF16), axis, pairs)
        from_left, from_right = next_left, next_right
    total = piece(partial_rows, here, size)
    if from_left is not None:
        total = total + from_left.astype(F32) + from_right.astype(F32)
    return total


def line_all_gather(own, axis):
    count = lax.axis_size(axis)
    here = lax.axis_index(axis)
    trees, size, width = own.shape
    lefts = [own]
    rights = [own]
    for step in range(1, count):
        pairs = [(i, i + 1) for i in range(step - 1, count - 1)]
        lefts.append(lax.ppermute(lefts[-1], axis, pairs))
        pairs = [(i, i - 1) for i in range(count - step, 0, -1)]
        rights.append(lax.ppermute(rights[-1], axis, pairs))
    result = jnp.zeros((trees, count * size, width), own.dtype)
    result = lax.dynamic_update_slice_in_dim(result, own, here * size, 1)
    for step in range(1, count):
        value = jnp.where(here >= step, lefts[step], rights[count - step])
        slot = lax.rem(here - step + count, count)
        result = lax.dynamic_update_slice_in_dim(result, value, slot * size, 1)
    return result


def earlier_gather(own, axis):
    count = lax.axis_size(axis)
    here = lax.axis_index(axis)
    trees, rows, width = own.shape
    result = jnp.zeros((trees, count * rows, width), own.dtype)
    result = lax.dynamic_update_slice_in_dim(result, own, here * rows, 1)
    for step in range(1, count):
        other = lax.ppermute(own, axis, [(i, i + step) for i in range(count - step)])
        slot = lax.rem(here - step + count, count)
        result = lax.dynamic_update_slice_in_dim(result, other, slot * rows, 1)
    return result


def earlier_return(full, axis):
    count = lax.axis_size(axis)
    here = lax.axis_index(axis)
    rows = full.shape[1] // count
    total = piece(full, here, rows)
    for step in range(1, count):
        slot = lax.rem(here - step + count, count)
        other = lax.ppermute(
            piece(full, slot, rows).astype(BF16),
            axis,
            [(i + step, i) for i in range(count - step)],
        )
        total = total + other.astype(F32)
    return total


def small_sum(values, axis):
    count = lax.axis_size(axis)
    total = values
    for step in range(1, count):
        total = total + lax.ppermute(
            values, axis, [(i, (i + step) % count) for i in range(count)]
        )
    return total


def norm_back(grad, values, gain):
    root = lax.rsqrt(jnp.mean(values * values, axis=-1, keepdims=True) + EPS)
    weighted = grad * gain
    mean = jnp.mean(weighted * values, axis=-1, keepdims=True)
    return root * weighted - values * (root * root * root) * mean


def on_device(
    tokens, norm_one, q_weight, k_weight, v_weight, o_weight, norm_two,
    gate_weight, up_weight, down_weight, segment_ids, parent_ids, path_pos, cotangent,
):
    ctx = lax.axis_index("context")
    ctx_count = lax.axis_size("context")
    ten = lax.axis_index("tensor")
    ten_count = lax.axis_size("tensor")
    tree_count, rows, width = tokens.shape
    share = rows // ten_count
    trees = tree_count // MICRO
    flat = trees * rows
    part, q_width = q_weight.shape
    kv_width = k_weight.shape[1]
    q_heads = q_width // HEAD
    kv_heads = kv_width // HEAD
    used = q_width + 2 * kv_width
    packed_width = round_up(used + 2, LANES)
    tree_len = rows * ctx_count

    attention_block = jnp.concatenate(
        [
            q_weight, k_weight, v_weight, norm_one[:, None], norm_two[:, None],
            jnp.zeros((part, packed_width - used - 2), BF16),
        ],
        axis=1,
    )
    attention_full = lax.all_gather(attention_block, WEIGHT_AXES, axis=0, tiled=True)
    o_full = lax.all_gather(o_weight.T, WEIGHT_AXES, axis=0, tiled=True)
    down_full = lax.all_gather(down_weight.T, WEIGHT_AXES, axis=0, tiled=True)
    gate_full = lax.all_gather(gate_weight, WEIGHT_AXES, axis=0, tiled=True)
    up_full = lax.all_gather(up_weight, WEIGHT_AXES, axis=0, tiled=True)
    gain_one = attention_full[:, used].astype(F32)
    gain_two = attention_full[:, used + 1].astype(F32)

    lane = np.arange(q_heads * LANES)
    column = np.arange(q_width)
    select = jnp.asarray(
        (lane[:, None] // LANES == column[None, :] // HEAD)
        & (lane[:, None] % LANES == column[None, :] % HEAD),
        BF16,
    )
    frequency = THETA ** (-(jnp.arange(HALF, dtype=F32) * 2.0 / HEAD))
    pad = jnp.zeros((flat, LANES - HEAD), F32)
    ctx_ref = jnp.reshape(ctx, (1,)).astype(jnp.int32)

    state = []
    for micro in range(MICRO):
        pick = slice(micro * trees, (micro + 1) * trees)
        m = {}
        state.append(m)
        m["x"] = tokens[pick]
        m["dy"] = cotangent[pick]
        seg, par, pos = segment_ids[pick], parent_ids[pick], path_pos[pick]

        def here(ids):
            return lax.dynamic_slice_in_dim(ids, ctx * rows, rows, 1)

        m["ids"] = (
            here(seg)[:, :, None], here(par)[:, :, None], here(pos)[:, :, None],
            seg[:, None, :], pos[:, None, :],
        )
        angles = here(pos).reshape(flat).astype(F32)[:, None] * frequency[None, :]
        cosine, sine = jnp.cos(angles), jnp.sin(angles)
        m["cos"] = jnp.concatenate([cosine, cosine, pad], axis=1)
        m["sin"] = jnp.concatenate([-sine, sine, pad], axis=1)
        x = m["x"].reshape(flat, width).astype(F32)
        m["root_one"] = lax.rsqrt(jnp.mean(x * x, axis=-1, keepdims=True) + EPS)
        m["x_here"] = lax.dynamic_slice_in_dim(m["x"], ten * share, share, 1).astype(F32)
        m["dy_here"] = lax.dynamic_slice_in_dim(m["dy"], ten * share, share, 1).astype(F32)

    for m in state:
        x = m["x"].reshape(flat, width).astype(F32)
        m["normed"] = (x * m["root_one"] * gain_one).astype(BF16)
        packed = mm(m["normed"], attention_full)
        m["q"], kv = split_heads(packed, m["cos"], m["sin"], q_heads, kv_heads, rows)
        m["kv"] = earlier_gather(kv.reshape(trees, rows, -1), "context")
    for m in state:
        wide = attend_forward(ctx_ref, m["q"], m["kv"], m["ids"], q_heads, kv_heads, rows)
        m["attended"] = mm(wide, select).astype(BF16)
        product = mm_nt(m["attended"], o_full).reshape(trees, rows, width)
        m["middle"] = m["x_here"] + line_reduce_scatter(product, share, "tensor")
    for m in state:
        middle = m["middle"]
        root = lax.rsqrt(jnp.mean(middle * middle, axis=-1, keepdims=True) + EPS)
        m["root_two"] = root
        m["normed_two"] = line_all_gather((middle * root * gain_two).astype(BF16), "tensor")

    for m in state:
        m["dmixed"] = mm(m["dy"].reshape(flat, width), down_full)
    for m in state:
        normed_two = m["normed_two"].reshape(flat, width)
        gate = mm(normed_two, gate_full)
        up = mm(normed_two, up_full)
        sigmoid = 1.0 / (1.0 + jnp.exp(-gate))
        silu = gate * sigmoid
        m["mixed"] = (silu * up).astype(BF16)
        slope = sigmoid * (1.0 + gate * (1.0 - sigmoid))
        m["dgate"] = (m["dmixed"] * up * slope).astype(BF16)
        m["dup"] = (m["dmixed"] * silu).astype(BF16)
        dn2 = mm_nt(m["dgate"], gate_full) + mm_nt(m["dup"], up_full)
        m["dn2"] = line_reduce_scatter(dn2.reshape(trees, rows, width), share, "tensor")
    for m in state:
        middle, dn2 = m["middle"], m["dn2"]
        m["gain_two_grad"] = jnp.sum(dn2 * middle * m["root_two"], axis=(0, 1))
        m["dmiddle"] = m["dy_here"] + norm_back(dn2, middle, gain_two)
        m["dmb"] = line_all_gather(m["dmiddle"].astype(BF16), "tensor").reshape(flat, width)
    for m in state:
        out = mm_nt(m["mixed"], down_full).reshape(trees, rows, width)
        m["out"] = (m["middle"] + line_reduce_scatter(out, share, "tensor")).astype(BF16)

    def together(name):
        return jnp.concatenate([m[name].reshape(flat, -1) for m in state], axis=0)

    def scattered(grad):
        return lax.psum_scatter(grad.astype(BF16), WEIGHT_AXES, scatter_dimension=0, tiled=True)

    dy_all = cotangent.reshape(-1, width)
    normed_two_all = together("normed_two")
    down_grad = scattered(mm_tn(dy_all, together("mixed")))
    gate_grad = scattered(mm_tn(normed_two_all, together("dgate")))
    up_grad = scattered(mm_tn(normed_two_all, together("dup")))

    for m in state:
        dattended = mm(m["dmb"], o_full).astype(BF16)
        do_wide = mm_nt(dattended, select).astype(BF16)
        dq, dk, dv = attend_backward(
            ctx_ref, m["q"], m["kv"], do_wide, m["ids"], q_heads, kv_heads, rows
        )
        dkv = earlier_return(jnp.concatenate([dk, dv], axis=2), "context").reshape(flat, -1)
        m["dqkv"] = pack_heads(
            dq, dkv, m["cos"], m["sin"], q_heads, kv_heads, packed_width, rows
        )
        dn1 = mm_nt(m["dqkv"], attention_full)
        x = m["x"].reshape(flat, width).astype(F32)
        m["gain_one_grad"] = jnp.sum(dn1 * x * m["root_one"], axis=0)
        m["dn1"] = line_reduce_scatter(dn1.reshape(trees, rows, width), share, "tensor")
    o_grad = scattered(mm_tn(together("dmb"), together("attended")))
    for m in state:
        m["dx"] = (m["dmiddle"] + norm_back(m["dn1"], m["x_here"], gain_one)).astype(BF16)

    attention_grad = mm_tn(together("normed"), together("dqkv"))
    gains = [sum(m[name] for m in state) for name in ("gain_one_grad", "gain_two_grad")]
    columns = lax.broadcasted_iota(jnp.int32, attention_grad.shape, 1)
    attention_grad = jnp.where(
        columns == used,
        gains[0][:, None],
        jnp.where(columns == used + 1, gains[1][:, None], attention_grad),
    )
    attention_grad = scattered(attention_grad).astype(F32)
    gain_grads = small_sum(attention_grad[:, used : used + 2], "tensor")
    return (
        jnp.concatenate([m["out"] for m in state], axis=0),
        jnp.concatenate([m["dx"] for m in state], axis=0),
        gain_grads[:, 0],
        attention_grad[:, :q_width],
        attention_grad[:, q_width : q_width + kv_width],
        attention_grad[:, q_width + kv_width : used],
        o_grad.T.astype(F32),
        gain_grads[:, 1],
        gate_grad.astype(F32),
        up_grad.astype(F32),
        down_grad.T.astype(F32),
    )


def solution(mesh):
    weights = ("fsdp", "context")
    return jax.shard_map(
        on_device,
        mesh=mesh,
        in_specs=(
            P("fsdp", "context", None),
            P(weights),
            P(weights, "tensor"),
            P(weights, "tensor"),
            P(weights, "tensor"),
            P("tensor", weights),
            P(weights),
            P(weights, "tensor"),
            P(weights, "tensor"),
            P("tensor", weights),
            P("fsdp", None),
            P("fsdp", None),
            P("fsdp", None),
            P("fsdp", "context", None),
        ),
        out_specs=(
            P("fsdp", ("context", "tensor"), None),
            P("fsdp", ("context", "tensor"), None),
            P(weights),
            P(weights, "tensor"),
            P(weights, "tensor"),
            P(weights, "tensor"),
            P("tensor", weights),
            P(weights),
            P(weights, "tensor"),
            P(weights, "tensor"),
            P("tensor", weights),
        ),
        check_vma=False,
    )
```

time: 2800 us -> 1270 us (0.45)
  waiting for transfers between devices: 1750 us -> 620 us
  matrix products: 428 us -> 239 us
  other arithmetic: 216 us -> 57.3 us
  local copies, waits for them, and re-layouts: 191 us -> 63.3 us
  starting transfers between devices: 68.6 us -> 182 us
  blocking collectives: 96.4 us -> 0 us
  Pallas kernels: 0 us -> 80.9 us
    psum x3 -> x0, waiting for transfers between devices: 1410 us -> none  [row_total(): total = lax.psum(partial_value, 'tensor')]
    ppermute x0 -> x79, waiting for transfers between devices: none -> 441 us  [the longest x24 167 us: line_reduce_scatter(): next_left = lax.ppermute(value.astype(BF16), axis, pairs)]
    dot_general x70 -> x27, matrix products: 428 us -> 239 us  [the longest x10 88.9 us: mm(): lax.dot_general(left, right, (((1,), (0,)), ((), ())), preferred_element_...]
    ppermute x0 -> x79, starting transfers between devices: none -> 182 us  [the longest x24 92.7 us: line_reduce_scatter(): next_left = lax.ppermute(value.astype(BF16), axis, pairs)]
    unnamed x24 -> x5, other arithmetic: 93.6 us -> 0.01 us
    pallas_call x0 -> x8, Pallas kernels: none -> 80.9 us  [the longest x2 36 us: attend_backward(): pl.pallas_call(functools.partial(backward_kernel, rows, tree_len, block,...]
    all_gather x5, waiting for transfers between devices: 125 us -> 52.2 us  [the longest x1 34.2 us: on_device(): lax.all_gather(attention_block, WEIGHT_AXES, axis=0, tiled=True)]
    all_to_all x16 -> x0, starting transfers between devices: 66.6 us -> none  [the longest x2 9.05 us: on_device(): lax.all_to_all(v_wide, 'context', split_axis=2, concat_axis=1, tiled=True)]
  transfers between devices with their start and end apart: 31 -> 89, of which waited for: 16 -> 50; matrix products, arithmetic and copies ran while one was open for 25% -> 17% of each run, Pallas kernels for 0% -> 3%
where the time goes in v1:
time: 1270 us; the launch traced here: 1260 us
  waiting for transfers between devices  620 us (49%)
  matrix products  239 us (19%)
  starting transfers between devices  182 us (14%)
  Pallas kernels  80.9 us (6%)
  local copies, waits for them, and re-layouts  63.3 us (5%)
  other arithmetic  57.3 us (5%)
  between operations  16.3 us (1%)
    ppermute x24, waiting for transfers between devices, line_reduce_scatter(): next_left = lax.ppermute(value.astype(BF16), axis, pairs)  167 us
    ppermute x12, waiting for transfers between devices, line_all_gather(): rights.append(lax.ppermute(rights[-1], axis, pairs))  133 us
    reduce_scatter x4, waiting for transfers between devices, scattered(): lax.psum_scatter(grad.astype(BF16), WEIGHT_AXES, scatter_dimension=0, til...  124 us
    ppermute x24, starting transfers between devices, line_reduce_scatter(): next_left = lax.ppermute(value.astype(BF16), axis, pairs)  92.7 us
    dot_general x10, matrix products, mm(): lax.dot_general(left, right, (((1,), (0,)), ((), ())), preferred_element_...  88.9 us
    dot_general x12, matrix products, mm_nt(): lax.dot_general(left, right, (((1,), (1,)), ((), ())), preferred_element_...  88.9 us
    ppermute x24, waiting for transfers between devices, line_reduce_scatter(): next_right = lax.ppermute(value.astype(BF16), axis, pairs)  77.2 us
    dot_general x5, matrix products, mm_tn(): lax.dot_general(left, right, (((0,), (0,)), ((), ())), preferred_element_...  61 us
  transfers between devices with their start and end apart: 89, of which 50 were waited for; matrix products, arithmetic and copies ran while one was open for 17% of the time, Pallas kernels for 3%

profile of v1, /device:TPU:0, one launch (start us, length us, event | category | flops | bytes accessed | tf_op | source)
XLA Modules:
  0.0 1258.9 jit_solution(17297658584457917480)
XLA Ops:
  22.5 34.2 %all-gather.6.cloned.1.call-done = bf16[2560,1024]{1,0:T(8,128)(2,1)} async-done(((bf16[320,1024]{1,0:T(8,128)(2,1)}), bf16[2560,1024]{1,0:T(8,128)(2,1)}) %all-gather.6.cloned.1.call-update) | async-done | bytes 5242896 | tf_op jit(solution)/shard_map/all_gather | solution.py:401
  79.6 16.1 %collective-permute-done.19 = bf16[1,512,512]{2,1,0:T(8,128)(2,1)S(1)} collective-permute-done((bf16[1,512,512]{2,1,0:T(8,128)(2,1)}, bf16[1,512,512]{2,1,0:T(8,128)(2,1)S(1)}, u32[]{:S(2)}, u32[]{:S(2)}) %collective-permute-start.19) | collective-permute-done | bytes 524320 | tf_op jit(solution)/shard_map/ppermute | solution.py:335
  96.8 12.7 %attend_forward.3 = bf16[512,1024]{1,0:T(8,128)(2,1)} custom-call(s32[1]{0:T(128)} %bitcast.ctx_ref, bf16[512,1024]{1,0:T(8,128)(2,1)} %get-tuple-element.23.q_ref, bf16[1,1024,512]{2,1,0:T(8,128)(2,1)} %copy-done.18, bf16[1,1024,512]{2,1,0:T(8,128)(2,1)} %copy-done.18, s32[1,512,1]{2,1,0:T(8,128)} %copy.78.seg_q, s32[1,512,1]{2,1,0:T(8,128)} %copy.79.par_q, ...), custom_call_target="tpu_custom_call" | custom-call | flops 2147483648 | bytes 4194304 | tf_op jit(solution)/shard_map/attend_forward/pallas_call | solution.py:237
  122.5 11.6 collective-permute-done.20
  140.0 11.5 collective-permute-done.21
  170.0 15.3 %collective-permute-done.25 = bf16[1,128,2560]{2,1,0:T(8,128)(2,1)S(1)} collective-permute-done((bf16[1,128,2560]{2,1,0:T(8,128)(2,1)S(1)}, bf16[1,128,2560]{2,1,0:T(8,128)(2,1)S(1)}, u32[]{:S(2)}, u32[]{:S(2)}) %collective-permute-start.25) | collective-permute-done | bytes 655392 | tf_op jit(solution)/shard_map/ppermute | solution.py:300
  206.6 12.0 collective-permute-done.28
  235.2 11.1 fusion.32
  246.3 12.5 fusion.145
  258.8 17.9 %all-gather.10.cloned.1.call-done = bf16[2560,1728]{1,0:T(8,128)(2,1)} async-done(((bf16[320,1728]{1,0:T(8,128)(2,1)}), bf16[2560,1728]{1,0:T(8,128)(2,1)}) %all-gather.10.cloned.1.call-update) | async-done | bytes 8847376 | tf_op jit(solution)/shard_map/all_gather | solution.py:404
  276.7 14.8 %multiply_convert_fusion = (bf16[512,1728]{0,1:T(8,128)(2,1)}, bf16[512,1728]{0,1:T(8,128)(2,1)S(1)}, bf16[512,1728]{0,1:T(8,128)(2,1)}) fusion(f32[512,1728]{0,1:T(8,128)} %fusion.32, f32[512,1728]{0,1:T(8,128)} %fusion.145, bf16[512,2560]{1,0:T(8,128)(2,1)} %bitcast_dynamic-update-slice_fusion.8, bf16[2560,1728]{1,0:T(8,128)(2,1)} %all-gather.10.cloned.1.call-done), kind=kOutput, calls=%fused_computation.41 | convolution fusion | flops 4543119360 | bytes 23855104 | tf_op jit(solution)/shard_map/dot_general | solution.py:31
  382.3 13.3 %collective-permute-done.34 = bf16[1,128,2560]{2,1,0:T(8,128)(2,1)S(1)} collective-permute-done((bf16[1,128,2560]{2,1,0:T(8,128)(2,1)S(1)}, bf16[1,128,2560]{2,1,0:T(8,128)(2,1)S(1)}, u32[]{:S(2)}, u32[]{:S(2)}) %collective-permute-start.34) | collective-permute-done | bytes 655392 | tf_op jit(solution)/shard_map/ppermute | solution.py:294
  412.7 13.2 %collective-permute-start.63 = (bf16[1,128,2560]{2,1,0:T(8,128)(2,1)S(1)}, bf16[1,128,2560]{2,1,0:T(8,128)(2,1)S(1)}, u32[]{:S(2)}, u32[]{:S(2)}) collective-permute-start(bf16[1,128,2560]{2,1,0:T(8,128)(2,1)S(1)} %get-tuple-element.98), channel_id=1, source_target_pairs={{0,1},{1,2},{2,3},{4,5},{5,6},{6,7},{8,9},{9,10},{10,11},{12,13},{... | collective-permute-start | bytes 1966088 | tf_op jit(solution)/shard_map/ppermute | solution.py:316
  425.8 11.0 collective-permute-done.64
  438.8 14.0 %collective-permute-done.65 = bf16[1,128,2560]{2,1,0:T(8,128)(2,1)S(1)} collective-permute-done((bf16[1,128,2560]{2,1,0:T(8,128)(2,1)S(1)}, bf16[1,128,2560]{2,1,0:T(8,128)(2,1)S(1)}, u32[]{:S(2)}, u32[]{:S(2)}) %collective-permute-start.65) | collective-permute-done | bytes 655392 | tf_op jit(solution)/shard_map/ppermute | solution.py:318
  454.8 13.1 %collective-permute-done.66 = bf16[1,128,2560]{2,1,0:T(8,128)(2,1)S(1)} collective-permute-done((bf16[1,128,2560]{2,1,0:T(8,128)(2,1)S(1)}, bf16[1,128,2560]{2,1,0:T(8,128)(2,1)S(1)}, u32[]{:S(2)}, u32[]{:S(2)}) %collective-permute-start.66) | collective-permute-done | bytes 655392 | tf_op jit(solution)/shard_map/ppermute | solution.py:318
  479.0 18.0 %attend_backward.3 = (bf16[512,1024]{1,0:T(8,128)(2,1)}, f32[1,1024,256]{2,1,0:T(8,128)}, f32[1,1024,256]{2,1,0:T(8,128)}) custom-call(s32[1]{0:T(128)} %bitcast.ctx_ref, bf16[512,1024]{1,0:T(8,128)(2,1)} %get-tuple-element.23.q_ref, bf16[1,1024,512]{2,1,0:T(8,128)(2,1)} %copy-done.18, bf16[1,1024,512]{2,1,0:T(8,128)(2,1)} %copy-done.18, ...), custom_call_target="tpu_custom_call" | custom-call | flops 5368709120 | bytes 6291456 | tf_op jit(solution)/shard_map/attend_backward/pallas_call | solution.py:262
  500.2 14.8 %collective-permute-done.69 = bf16[1,512,512]{2,1,0:T(8,128)(2,1)S(1)} collective-permute-done((bf16[1,512,512]{2,1,0:T(8,128)(2,1)S(1)}, bf16[1,512,512]{2,1,0:T(8,128)(2,1)S(1)}, u32[]{:S(2)}, u32[]{:S(2)}) %collective-permute-start.69) | collective-permute-done | bytes 524320 | tf_op jit(solution)/shard_map/ppermute | solution.py:348
  553.9 12.6 attend_forward.2
  611.1 21.2 %collective-permute-done.6 = bf16[1,128,2560]{2,1,0:T(8,128)(2,1)S(1)} collective-permute-done((bf16[1,128,2560]{2,1,0:T(8,128)(2,1)S(1)}, bf16[1,128,2560]{2,1,0:T(8,128)(2,1)S(1)}, u32[]{:S(2)}, u32[]{:S(2)}) %collective-permute-start.6) | collective-permute-done | bytes 655392 | tf_op jit(solution)/shard_map/ppermute | solution.py:300
  640.6 13.2 %collective-permute-done.8 = bf16[1,128,2560]{2,1,0:T(8,128)(2,1)S(1)} collective-permute-done((bf16[1,128,2560]{2,1,0:T(8,128)(2,1)S(1)}, bf16[1,128,2560]{2,1,0:T(8,128)(2,1)S(1)}, u32[]{:S(2)}, u32[]{:S(2)}) %collective-permute-start.8) | collective-permute-done | bytes 655392 | tf_op jit(solution)/shard_map/ppermute | solution.py:318
  655.8 16.2 %collective-permute-done.9 = bf16[1,128,2560]{2,1,0:T(8,128)(2,1)S(1)} collective-permute-done((bf16[1,128,2560]{2,1,0:T(8,128)(2,1)S(1)}, bf16[1,128,2560]{2,1,0:T(8,128)(2,1)S(1)}, u32[]{:S(2)}, u32[]{:S(2)}) %collective-permute-start.9) | collective-permute-done | bytes 655392 | tf_op jit(solution)/shard_map/ppermute | solution.py:318
  695.2 14.7 %multiply_convert_fusion.2 = (bf16[512,1728]{0,1:T(8,128)(2,1)}, bf16[512,1728]{0,1:T(8,128)(2,1)}, bf16[512,1728]{0,1:T(8,128)(2,1)}) fusion(f32[512,1728]{0,1:T(8,128)} %fusion.34, f32[512,1728]{0,1:T(8,128)} %fusion.141, bf16[512,2560]{1,0:T(8,128)(2,1)S(1)} %bitcast_dynamic-update-slice_fusion.12, bf16[2560,1728]{1,0:T(8,128)(2,1)} %all-gather.10.cloned.1.call-done), kind=kOutput, calls=%fused_computation.43 | convolution fusion | flops 4543119360 | bytes 23855104 | tf_op jit(solution)/shard_map/dot_general | solution.py:31
  831.7 12.5 collective-permute-done.45
  887.4 18.0 %attend_backward.2 = (bf16[512,1024]{1,0:T(8,128)(2,1)}, f32[1,1024,256]{2,1,0:T(8,128)}, f32[1,1024,256]{2,1,0:T(8,128)}) custom-call(s32[1]{0:T(128)} %bitcast.ctx_ref, bf16[512,1024]{1,0:T(8,128)(2,1)} %get-tuple-element.21.q_ref, bf16[1,1024,512]{2,1,0:T(8,128)(2,1)} %copy-done.19, bf16[1,1024,512]{2,1,0:T(8,128)(2,1)} %copy-done.19, ...), custom_call_target="tpu_custom_call" | custom-call | flops 5368709120 | bytes 6291456 | tf_op jit(solution)/shard_map/attend_backward/pallas_call | solution.py:262
  909.4 24.8 %collective-permute-done.50 = bf16[1,512,512]{2,1,0:T(8,128)(2,1)S(1)} collective-permute-done((bf16[1,512,512]{2,1,0:T(8,128)(2,1)S(1)}, bf16[1,512,512]{2,1,0:T(8,128)(2,1)S(1)}, u32[]{:S(2)}, u32[]{:S(2)}) %collective-permute-start.50) | collective-permute-done | bytes 524320 | tf_op jit(solution)/shard_map/ppermute | solution.py:348
  957.3 14.6 %fusion = bf16[2560,1728]{0,1:T(8,128)(2,1)} fusion(bf16[1024,2560]{1,0:T(8,128)(2,1)} %bitcast.360, bf16[512,1728]{0,1:T(8,128)(2,1)} %get-tuple-element.110, bf16[512,1728]{0,1:T(8,128)(2,1)} %get-tuple-element.107), kind=kOutput, calls=%fused_computation.4 | convolution fusion | flops 9071198208 | bytes 17629184 | tf_op jit(solution)/shard_map/dot_general | solution.py:39
  971.9 12.8 %copy.90 = bf16[2560,1728]{1,0:T(8,128)(2,1)} copy(bf16[2560,1728]{0,1:T(8,128)(2,1)} %fusion) | data formatting | bytes 17694720
  984.9 15.0 %convolution_convert_fusion.2 = bf16[2560,1728]{1,0:T(8,128)(2,1)} fusion(bf16[512,1728]{0,1:T(8,128)(2,1)} %copy-done.33, bf16[512,1728]{0,1:T(8,128)(2,1)} %get-tuple-element.106, bf16[512,2560]{1,0:T(8,128)(2,1)} %bitcast_dynamic-update-slice_fusion.8, bf16[512,2560]{1,0:T(8,128)(2,1)} %copy-done.8), kind=kOutput, calls=%fused_computation.2 | convolution fusion | flops 9081683968 | bytes 17629184 | tf_op jit(solution)/shard_map/dot_general | solution.py:39
  1000.0 15.4 %convolution_convert_fusion.1 = bf16[2560,1728]{1,0:T(8,128)(2,1)} fusion(bf16[512,1728]{0,1:T(8,128)(2,1)} %get-tuple-element.108, bf16[512,1728]{0,1:T(8,128)(2,1)} %get-tuple-element.105, bf16[512,2560]{1,0:T(8,128)(2,1)} %bitcast_dynamic-update-slice_fusion.8, bf16[512,2560]{1,0:T(8,128)(2,1)} %copy-done.8), kind=kOutput, calls=%fused_computation.1 | convolution fusion | flops 9081683968 | bytes 17629184 | tf_op jit(solution)/shard_map/dot_general | solution.py:39
  1121.9 48.3 %reduce-scatter.12.cloned.1.call-done = bf16[320,1728]{1,0:T(8,128)(2,1)} async-done(((bf16[2560,1728]{1,0:T(8,128)(2,1)}), bf16[320,1728]{1,0:T(8,128)(2,1)}) %reduce-scatter.12.cloned.1.call-update) | async-done | bytes 1105936 | tf_op jit(solution)/shard_map/reduce_scatter | solution.py:489
  1172.9 76.1 %reduce-scatter.14.cloned.1.call-done = bf16[320,1728]{1,0:T(8,128)(2,1)} async-done(((bf16[2560,1728]{1,0:T(8,128)(2,1)}), bf16[320,1728]{1,0:T(8,128)(2,1)}) %reduce-scatter.14.cloned.1.call-update) | async-done | bytes 1105936 | tf_op jit(solution)/shard_map/reduce_scatter | solution.py:489
  (424 shorter events, 660.2 us)
Async XLA Ops:
  7.2 49.6 %all-gather.6.cloned.1.call-start = ((), (), s32[]{:S(2)}) async-start(), calls=%async_computation.5 | async-start | bytes 5898240 | tf_op jit(solution)/shard_map/all_gather | solution.py:401
  12.9 99.0 %all-gather.8.cloned.1.call-start = ((), (), s32[]{:S(2)}) async-start(), calls=%async_computation.6 | async-start | bytes 3686400 | tf_op jit(solution)/shard_map/all_gather | solution.py:402
  13.6 221.6 %all-gather.14.cloned.1.call-start = ((), (), s32[]{:S(2)}) async-start(), calls=%async_computation.9 | async-start | bytes 10321920 | tf_op jit(solution)/shard_map/all_gather | solution.py:403
  14.4 231.9 %all-gather.12.cloned.1.call-start = ((), (), s32[]{:S(2)}) async-start(), calls=%async_computation.8 | async-start | bytes 10321920 | tf_op jit(solution)/shard_map/all_gather | solution.py:405
  15.0 261.7 %all-gather.10.cloned.1.call-start = ((), (), s32[]{:S(2)}) async-start(), calls=%async_computation.7 | async-start | bytes 10321920 | tf_op jit(solution)/shard_map/all_gather | solution.py:404
  15.6 1082.9 %reduce-scatter.10.cloned.1.call-start = ((), (), s32[]{:S(2)}) async-start(), calls=%async_computation.11 | async-start | bytes 3686400 | tf_op jit(solution)/shard_map/reduce_scatter | solution.py:489
  160.7 24.6 %collective-permute-start.25 = (bf16[1,128,2560]{2,1,0:T(8,128)(2,1)S(1)}, bf16[1,128,2560]{2,1,0:T(8,128)(2,1)S(1)}, u32[]{:S(2)}, u32[]{:S(2)}) collective-permute-start(bf16[1,128,2560]{2,1,0:T(8,128)(2,1)S(1)} %fusion.84), channel_id=1, source_target_pairs={{3,2},{2,1},{1,0},{7,6},{6,5},{5,4},{11,10},{10,9},{9,8},{15,14},{... | collective-permute-start | bytes 1966088 | tf_op jit(solution)/shard_map/ppermute | solution.py:300
  311.1 33.7 %collective-permute-start.60 = (bf16[1,128,2560]{2,1,0:T(8,128)(2,1)S(1)}, bf16[1,128,2560]{2,1,0:T(8,128)(2,1)S(1)}, u32[]{:S(2)}, u32[]{:S(2)}) collective-permute-start(bf16[1,128,2560]{2,1,0:T(8,128)(2,1)S(1)} %get-tuple-element.138), channel_id=1, source_target_pairs={{3,2},{7,6},{11,10},{15,14},{19,18},{23,22},{27,26},{31,30}} | collective-permute-start | bytes 1966088 | tf_op jit(solution)/shard_map/ppermute | solution.py:300
  321.2 39.5 %collective-permute-start.35 = (bf16[1,128,2560]{2,1,0:T(8,128)(2,1)S(1)}, bf16[1,128,2560]{2,1,0:T(8,128)(2,1)S(1)}, u32[]{:S(2)}, u32[]{:S(2)}) collective-permute-start(bf16[1,128,2560]{2,1,0:T(8,128)(2,1)S(1)} %get-tuple-element.142), channel_id=1, source_target_pairs={{3,2},{7,6},{11,10},{15,14},{19,18},{23,22},{27,26},{31,30}} | collective-permute-start | bytes 1966088 | tf_op jit(solution)/shard_map/ppermute | solution.py:300
  326.3 27.9 %collective-permute-start.58 = (bf16[1,128,2560]{2,1,0:T(8,128)(2,1)S(1)}, bf16[1,128,2560]{2,1,0:T(8,128)(2,1)S(1)}, u32[]{:S(2)}, u32[]{:S(2)}) collective-permute-start(bf16[1,128,2560]{2,1,0:T(8,128)(2,1)S(1)} %fusion.62), channel_id=1, source_target_pairs={{0,1},{1,2},{4,5},{5,6},{8,9},{9,10},{12,13},{13,14},{16,17},{17,1... | collective-permute-start | bytes 1966088 | tf_op jit(solution)/shard_map/ppermute | solution.py:294
  340.3 27.9 %collective-permute-start.33 = (bf16[1,128,2560]{2,1,0:T(8,128)(2,1)S(1)}, bf16[1,128,2560]{2,1,0:T(8,128)(2,1)S(1)}, u32[]{:S(2)}, u32[]{:S(2)}) collective-permute-start(bf16[1,128,2560]{2,1,0:T(8,128)(2,1)S(1)} %fusion.78), channel_id=1, source_target_pairs={{0,1},{1,2},{4,5},{5,6},{8,9},{9,10},{12,13},{13,14},{16,17},{17,1... | collective-permute-start | bytes 1966088 | tf_op jit(solution)/shard_map/ppermute | solution.py:294
  355.4 26.9 %collective-permute-start.59 = (bf16[1,128,2560]{2,1,0:T(8,128)(2,1)S(1)}, bf16[1,128,2560]{2,1,0:T(8,128)(2,1)S(1)}, u32[]{:S(2)}, u32[]{:S(2)}) collective-permute-start(bf16[1,128,2560]{2,1,0:T(8,128)(2,1)S(1)} %get-tuple-element.135), channel_id=1, source_target_pairs={{0,1},{1,2},{2,3},{4,5},{5,6},{6,7},{8,9},{9,10},{10,11},{12,13},{... | collective-permute-start | bytes 1966088 | tf_op jit(solution)/shard_map/ppermute | solution.py:294
  369.3 26.3 %collective-permute-start.34 = (bf16[1,128,2560]{2,1,0:T(8,128)(2,1)S(1)}, bf16[1,128,2560]{2,1,0:T(8,128)(2,1)S(1)}, u32[]{:S(2)}, u32[]{:S(2)}) collective-permute-start(bf16[1,128,2560]{2,1,0:T(8,128)(2,1)S(1)} %get-tuple-element.139), channel_id=1, source_target_pairs={{0,1},{1,2},{2,3},{4,5},{5,6},{6,7},{8,9},{9,10},{10,11},{12,13},{... | collective-permute-start | bytes 1966088 | tf_op jit(solution)/shard_map/ppermute | solution.py:294
  376.0 30.1 %collective-permute-start.37 = (bf16[1,128,2560]{2,1,0:T(8,128)(2,1)S(1)}, bf16[1,128,2560]{2,1,0:T(8,128)(2,1)S(1)}, u32[]{:S(2)}, u32[]{:S(2)}) collective-permute-start(bf16[1,128,2560]{2,1,0:T(8,128)(2,1)S(1)} %fusion.77), channel_id=1, source_target_pairs={{3,2},{2,1},{1,0},{7,6},{6,5},{5,4},{11,10},{10,9},{9,8},{15,14},{... | collective-permute-start | bytes 1966088 | tf_op jit(solution)/shard_map/ppermute | solution.py:300
  411.4 25.4 %collective-permute-start.64 = (bf16[1,128,2560]{2,1,0:T(8,128)(2,1)S(1)}, bf16[1,128,2560]{2,1,0:T(8,128)(2,1)S(1)}, u32[]{:S(2)}, u32[]{:S(2)}) collective-permute-start(bf16[1,128,2560]{2,1,0:T(8,128)(2,1)S(1)} %get-tuple-element.98), channel_id=1, source_target_pairs={{3,2},{2,1},{1,0},{7,6},{6,5},{5,4},{11,10},{10,9},{9,8},{15,14},{... | collective-permute-start | bytes 1966088 | tf_op jit(solution)/shard_map/ppermute | solution.py:318
  412.7 25.4 %collective-permute-start.63 = (bf16[1,128,2560]{2,1,0:T(8,128)(2,1)S(1)}, bf16[1,128,2560]{2,1,0:T(8,128)(2,1)S(1)}, u32[]{:S(2)}, u32[]{:S(2)}) collective-permute-start(bf16[1,128,2560]{2,1,0:T(8,128)(2,1)S(1)} %get-tuple-element.98), channel_id=1, source_target_pairs={{0,1},{1,2},{2,3},{4,5},{5,6},{6,7},{8,9},{9,10},{10,11},{12,13},{... | collective-permute-start | bytes 1966088 | tf_op jit(solution)/shard_map/ppermute | solution.py:316
  603.2 29.1 %collective-permute-start.6 = (bf16[1,128,2560]{2,1,0:T(8,128)(2,1)S(1)}, bf16[1,128,2560]{2,1,0:T(8,128)(2,1)S(1)}, u32[]{:S(2)}, u32[]{:S(2)}) collective-permute-start(bf16[1,128,2560]{2,1,0:T(8,128)(2,1)S(1)} %fusion.96), channel_id=1, source_target_pairs={{3,2},{2,1},{1,0},{7,6},{6,5},{5,4},{11,10},{10,9},{9,8},{15,14},{... | collective-permute-start | bytes 1966088 | tf_op jit(solution)/shard_map/ppermute | solution.py:300
  655.1 27.4 %collective-permute-start.11 = (bf16[1,128,2560]{2,1,0:T(8,128)(2,1)S(1)}, bf16[1,128,2560]{2,1,0:T(8,128)(2,1)S(1)}, u32[]{:S(2)}, u32[]{:S(2)}) collective-permute-start(bf16[1,128,2560]{2,1,0:T(8,128)(2,1)S(1)} %collective-permute-done.7), channel_id=1, source_target_pairs={{1,2},{2,3},{5,6},{6,7},{9,10},{10,11},{13,14},{14,15},{17,18},{18... | collective-permute-start | bytes 1966088 | tf_op jit(solution)/shard_map/ppermute | solution.py:316
  729.4 33.7 %collective-permute-start.41 = (bf16[1,128,2560]{2,1,0:T(8,128)(2,1)S(1)}, bf16[1,128,2560]{2,1,0:T(8,128)(2,1)S(1)}, u32[]{:S(2)}, u32[]{:S(2)}) collective-permute-start(bf16[1,128,2560]{2,1,0:T(8,128)(2,1)S(1)} %get-tuple-element.120), channel_id=1, source_target_pairs={{3,2},{7,6},{11,10},{15,14},{19,18},{23,22},{27,26},{31,30}} | collective-permute-start | bytes 1966088 | tf_op jit(solution)/shard_map/ppermute | solution.py:300
  739.3 39.3 %collective-permute-start.16 = (bf16[1,128,2560]{2,1,0:T(8,128)(2,1)S(1)}, bf16[1,128,2560]{2,1,0:T(8,128)(2,1)S(1)}, u32[]{:S(2)}, u32[]{:S(2)}) collective-permute-start(bf16[1,128,2560]{2,1,0:T(8,128)(2,1)S(1)} %get-tuple-element.128), channel_id=1, source_target_pairs={{3,2},{7,6},{11,10},{15,14},{19,18},{23,22},{27,26},{31,30}} | collective-permute-start | bytes 1966088 | tf_op jit(solution)/shard_map/ppermute | solution.py:300
  744.6 27.9 %collective-permute-start.39 = (bf16[1,128,2560]{2,1,0:T(8,128)(2,1)S(1)}, bf16[1,128,2560]{2,1,0:T(8,128)(2,1)S(1)}, u32[]{:S(2)}, u32[]{:S(2)}) collective-permute-start(bf16[1,128,2560]{2,1,0:T(8,128)(2,1)S(1)} %fusion.73), channel_id=1, source_target_pairs={{0,1},{1,2},{4,5},{5,6},{8,9},{9,10},{12,13},{13,14},{16,17},{17,1... | collective-permute-start | bytes 1966088 | tf_op jit(solution)/shard_map/ppermute | solution.py:294
  758.6 27.9 %collective-permute-start.14 = (bf16[1,128,2560]{2,1,0:T(8,128)(2,1)S(1)}, bf16[1,128,2560]{2,1,0:T(8,128)(2,1)S(1)}, u32[]{:S(2)}, u32[]{:S(2)}) collective-permute-start(bf16[1,128,2560]{2,1,0:T(8,128)(2,1)S(1)} %fusion.90), channel_id=1, source_target_pairs={{0,1},{1,2},{4,5},{5,6},{8,9},{9,10},{12,13},{13,14},{16,17},{17,1... | collective-permute-start | bytes 1966088 | tf_op jit(solution)/shard_map/ppermute | solution.py:294
  794.3 25.7 %collective-permute-start.18 = (bf16[1,128,2560]{2,1,0:T(8,128)(2,1)S(1)}, bf16[1,128,2560]{2,1,0:T(8,128)(2,1)S(1)}, u32[]{:S(2)}, u32[]{:S(2)}) collective-permute-start(bf16[1,128,2560]{2,1,0:T(8,128)(2,1)S(1)} %fusion.89), channel_id=1, source_target_pairs={{3,2},{2,1},{1,0},{7,6},{6,5},{5,4},{11,10},{10,9},{9,8},{15,14},{... | collective-permute-start | bytes 1966088 | tf_op jit(solution)/shard_map/ppermute | solution.py:300
  879.0 221.4 %reduce-scatter.8.cloned.1.call-start = ((), (), s32[]{:S(2)}) async-start(), calls=%async_computation.10 | async-start | bytes 5898240 | tf_op jit(solution)/shard_map/reduce_scatter | solution.py:489
  907.7 26.5 %collective-permute-start.50 = (bf16[1,512,512]{2,1,0:T(8,128)(2,1)S(1)}, bf16[1,512,512]{2,1,0:T(8,128)(2,1)S(1)}, u32[]{:S(2)}, u32[]{:S(2)}) collective-permute-start(bf16[1,512,512]{2,1,0:T(8,128)(2,1)S(1)} %dynamic-slice_convert_fusion.17), channel_id=1, source_target_pairs={{4,0},{5,1},{6,2},{7,3},{12,8},{13,9},{14,10},{15,11},{20,16},{21,... | collective-permute-start | bytes 1572872 | tf_op jit(solution)/shard_map/ppermute | solution.py:348
  957.2 158.5 %reduce-scatter.16.cloned.1.call-start = ((), (), s32[]{:S(2)}) async-start(), calls=%async_computation.14 | async-start | bytes 10321920
  984.7 185.4 %reduce-scatter.12.cloned.1.call-start = ((), (), s32[]{:S(2)}) async-start(), calls=%async_computation.12 | async-start | bytes 10321920 | tf_op jit(solution)/shard_map/reduce_scatter | solution.py:489
  1000.0 249.0 %reduce-scatter.14.cloned.1.call-start = ((), (), s32[]{:S(2)}) async-start(), calls=%async_computation.13 | async-start | bytes 10321920 | tf_op jit(solution)/shard_map/reduce_scatter | solution.py:489
  1020.9 24.8 %collective-permute-start.70 = (bf16[1,128,2560]{2,1,0:T(8,128)(2,1)S(1)}, bf16[1,128,2560]{2,1,0:T(8,128)(2,1)S(1)}, u32[]{:S(2)}, u32[]{:S(2)}) collective-permute-start(bf16[1,128,2560]{2,1,0:T(8,128)(2,1)S(1)} %get-tuple-element.123), channel_id=1, source_target_pairs={{0,1},{4,5},{8,9},{12,13},{16,17},{20,21},{24,25},{28,29}} | collective-permute-start | bytes 1966088 | tf_op jit(solution)/shard_map/ppermute | solution.py:294
  1022.2 34.2 %collective-permute-start.73 = (bf16[1,128,2560]{2,1,0:T(8,128)(2,1)S(1)}, bf16[1,128,2560]{2,1,0:T(8,128)(2,1)S(1)}, u32[]{:S(2)}, u32[]{:S(2)}) collective-permute-start(bf16[1,128,2560]{2,1,0:T(8,128)(2,1)S(1)} %get-tuple-element.124), channel_id=1, source_target_pairs={{3,2},{7,6},{11,10},{15,14},{19,18},{23,22},{27,26},{31,30}} | collective-permute-start | bytes 1966088 | tf_op jit(solution)/shard_map/ppermute | solution.py:300
  1023.0 28.7 %collective-permute-start.54 = (bf16[1,128,2560]{2,1,0:T(8,128)(2,1)S(1)}, bf16[1,128,2560]{2,1,0:T(8,128)(2,1)S(1)}, u32[]{:S(2)}, u32[]{:S(2)}) collective-permute-start(bf16[1,128,2560]{2,1,0:T(8,128)(2,1)S(1)} %get-tuple-element.114), channel_id=1, source_target_pairs={{3,2},{7,6},{11,10},{15,14},{19,18},{23,22},{27,26},{31,30}} | collective-permute-start | bytes 1966088 | tf_op jit(solution)/shard_map/ppermute | solution.py:300
  1063.3 25.7 %collective-permute-start.72 = (bf16[1,128,2560]{2,1,0:T(8,128)(2,1)S(1)}, bf16[1,128,2560]{2,1,0:T(8,128)(2,1)S(1)}, u32[]{:S(2)}, u32[]{:S(2)}) collective-permute-start(bf16[1,128,2560]{2,1,0:T(8,128)(2,1)S(1)} %get-tuple-element.121), channel_id=1, source_target_pairs={{0,1},{1,2},{2,3},{4,5},{5,6},{6,7},{8,9},{9,10},{10,11},{12,13},{... | collective-permute-start | bytes 1966088 | tf_op jit(solution)/shard_map/ppermute | solution.py:294
  (105 other events, 1919.9 us)
Sparse Core Ops, SparseCore 0:
  13.0 43.7 all-gather.5
  58.6 37.1 all-gather.7
  97.7 60.2 all-gather.13
  159.8 57.5 all-gather.11
  219.1 57.5 all-gather.9
  879.1 54.4 reduce-scatter.9
  957.4 54.6 reduce-scatter.7
  1015.7 75.3 reduce-scatter.15
  1094.8 75.3 reduce-scatter.11
  1173.6 75.3 reduce-scatter.13

commit v2 on v1

--- a/solution.py
+++ b/solution.py
@@ -6,6 +6,7 @@
 from jax import lax
 from jax.experimental import pallas as pl
 from jax.experimental.pallas import tpu as pltpu
+from jax.experimental.layout import Layout, with_layout_constraint
 from jax.sharding import PartitionSpec as P
 
 HEADS = 32
@@ -21,6 +22,10 @@
 WEIGHT_AXES = ("fsdp", "context")
 BF16 = jnp.bfloat16
 F32 = jnp.float32
+
+
+def row_major(value):
+    return with_layout_constraint(value, Layout(major_to_minor=(0, 1)))
 
 
 def round_up(value, unit):
@@ -280,78 +285,148 @@
     return lax.dynamic_slice_in_dim(values, index * size, size, 1)
 
 
-def line_reduce_scatter(partial_rows, size, axis):
-    count = lax.axis_size(axis)
-    here = lax.axis_index(axis)
-    from_left = None
-    from_right = None
-    for step in range(1, count):
-        index = jnp.clip(count - step + here, 0, count - 1)
-        value = piece(partial_rows, index, size)
-        if from_left is not None:
-            value = value + from_left.astype(F32)
-        pairs = [(i, i + 1) for i in range(step)]
-        next_left = lax.ppermute(value.astype(BF16), axis, pairs)
-        index = jnp.clip(here - (count - step), 0, count - 1)
-        value = piece(partial_rows, index, size)
-        if from_right is not None:
-            value = value + from_right.astype(F32)
-        pairs = [(count - 1 - i, count - 2 - i) for i in range(step)]
-        next_right = lax.ppermute(value.astype(BF16), axis, pairs)
-        from_left, from_right = next_left, next_right
-    total = piece(partial_rows, here, size)
-    if from_left is not None:
-        total = total + from_left.astype(F32) + from_right.astype(F32)
-    return total
-
-
-def line_all_gather(own, axis):
-    count = lax.axis_size(axis)
-    here = lax.axis_index(axis)
-    trees, size, width = own.shape
-    lefts = [own]
-    rights = [own]
-    for step in range(1, count):
-        pairs = [(i, i + 1) for i in range(step - 1, count - 1)]
-        lefts.append(lax.ppermute(lefts[-1], axis, pairs))
-        pairs = [(i, i - 1) for i in range(count - step, 0, -1)]
-        rights.append(lax.ppermute(rights[-1], axis, pairs))
-    result = jnp.zeros((trees, count * size, width), own.dtype)
-    result = lax.dynamic_update_slice_in_dim(result, own, here * size, 1)
-    for step in range(1, count):
-        value = jnp.where(here >= step, lefts[step], rights[count - step])
-        slot = lax.rem(here - step + count, count)
-        result = lax.dynamic_update_slice_in_dim(result, value, slot * size, 1)
-    return result
-
-
-def earlier_gather(own, axis):
-    count = lax.axis_size(axis)
-    here = lax.axis_index(axis)
-    trees, rows, width = own.shape
-    result = jnp.zeros((trees, count * rows, width), own.dtype)
-    result = lax.dynamic_update_slice_in_dim(result, own, here * rows, 1)
-    for step in range(1, count):
-        other = lax.ppermute(own, axis, [(i, i + step) for i in range(count - step)])
-        slot = lax.rem(here - step + count, count)
-        result = lax.dynamic_update_slice_in_dim(result, other, slot * rows, 1)
-    return result
-
-
-def earlier_return(full, axis):
-    count = lax.axis_size(axis)
-    here = lax.axis_index(axis)
-    rows = full.shape[1] // count
-    total = piece(full, here, rows)
-    for step in range(1, count):
-        slot = lax.rem(here - step + count, count)
-        other = lax.ppermute(
-            piece(full, slot, rows).astype(BF16),
-            axis,
-            [(i + step, i) for i in range(count - step)],
-        )
-        total = total + other.astype(F32)
-    return total
+class LineSum:
+    def __init__(self, values, size, axis):
+        self.values, self.size, self.axis = values, size, axis
+        self.count = lax.axis_size(axis)
+        self.here = lax.axis_index(axis)
+        self.step = 0
+        self.got = None
+
+    def sends(self):
+        self.step += 1
+        step, count = self.step, self.count
+        away = count - step
+        rights = [(i, i + 1) for i in range(step)]
+        lefts = [(count - 1 - i, count - 2 - i) for i in range(step)]
+        found = []
+        for side, pairs in ((0, rights), (1, lefts)):
+            index = jnp.clip(self.here + (away, -away)[side], 0, count - 1)
+            value = piece(self.values, index, self.size)
+            if self.got is not None:
+                value = value + self.got[side].astype(F32)
+            found.append((value.astype(BF16), self.axis, pairs))
+        return found
+
+    def receive(self, results):
+        self.got = results
+
+    def result(self):
+        assert self.step == self.count - 1
+        total = piece(self.values, self.here, self.size)
+        for other in self.got or ():
+            total = total + other.astype(F32)
+        return total
+
+
+class LineGather:
+    def __init__(self, own, axis):
+        self.own, self.axis = own, axis
+        self.count = lax.axis_size(axis)
+        self.here = lax.axis_index(axis)
+        self.lefts, self.rights = [own], [own]
+
+    def sends(self):
+        step, count = len(self.lefts), self.count
+        return [
+            (self.lefts[-1], self.axis, [(i, i + 1) for i in range(step - 1, count - 1)]),
+            (self.rights[-1], self.axis, [(i, i - 1) for i in range(count - step, 0, -1)]),
+        ]
+
+    def receive(self, results):
+        self.lefts.append(results[0])
+        self.rights.append(results[1])
+
+    def result(self):
+        count, here, own = self.count, self.here, self.own
+        assert len(self.lefts) == count
+        trees, size, width = own.shape
+        result = jnp.zeros((trees, count * size, width), own.dtype)
+        result = lax.dynamic_update_slice_in_dim(result, own, here * size, 1)
+        for step in range(1, count):
+            value = jnp.where(here >= step, self.lefts[step], self.rights[count - step])
+            slot = lax.rem(here - step + count, count)
+            result = lax.dynamic_update_slice_in_dim(result, value, slot * size, 1)
+        return result
+
+
+class EarlierGather:
+    def __init__(self, own, axis):
+        self.own, self.axis = own, axis
+        self.count = lax.axis_size(axis)
+
+    def sends(self):
+        count = self.count
+        return [
+            (self.own, self.axis, [(i, i + step) for i in range(count - step)])
+            for step in range(1, count)
+        ]
+
+    def receive(self, results):
+        self.others = results
+
+    def result(self):
+        count, own = self.count, self.own
+        here = lax.axis_index(self.axis)
+        trees, rows, width = own.shape
+        result = jnp.zeros((trees, count * rows, width), own.dtype)
+        result = lax.dynamic_update_slice_in_dim(result, own, here * rows, 1)
+        for step, other in enumerate(self.others, 1):
+            slot = lax.rem(here - step + count, count)
+            result = lax.dynamic_update_slice_in_dim(result, other, slot * rows, 1)
+        return result
+
+
+class EarlierReturn:
+    def __init__(self, full, axis):
+        self.full, self.axis = full, axis
+        self.count = lax.axis_size(axis)
+        self.rows = full.shape[1] // self.count
+
+    def sends(self):
+        count = self.count
+        here = lax.axis_index(self.axis)
+        found = []
+        for step in range(1, count):
+            slot = lax.rem(here - step + count, count)
+            value = piece(self.full, slot, self.rows).astype(BF16)
+            found.append((value, self.axis, [(i + step, i) for i in range(count - step)]))
+        return found
+
+    def receive(self, results):
+        self.others = results
+
+    def result(self):
+        total = piece(self.full, lax.axis_index(self.axis), self.rows)
+        for other in self.others:
+            total = total + other.astype(F32)
+        return total
+
+
+class Stages:
+    def __init__(self):
+        self.token = ()
+
+    def wait_for(self, *values):
+        self.token += values
+
+    def __call__(self, transfers, compute=None, inputs=()):
+        transfers = [t for t in transfers if getattr(t, "count", 2) > 1]
+        groups = [t.sends() for t in transfers]
+        values = [value for group in groups for value, _, _ in group]
+        tied = lax.optimization_barrier((*values, *inputs, *self.token))
+        token, at = [], 0
+        for transfer, group in zip(transfers, groups):
+            results = []
+            for _, axis, pairs in group:
+                results.append(lax.ppermute(tied[at], axis, pairs))
+                at += 1
+            transfer.receive(results)
+            token += results
+        outs = compute(*tied[at : at + len(inputs)]) if compute else ()
+        token += [o for o in outs]
+        self.token = tuple(token)
+        return outs
 
 
 def small_sum(values, axis):
@@ -442,85 +517,205 @@
         m["x_here"] = lax.dynamic_slice_in_dim(m["x"], ten * share, share, 1).astype(F32)
         m["dy_here"] = lax.dynamic_slice_in_dim(m["dy"], ten * share, share, 1).astype(F32)
 
-    for m in state:
-        x = m["x"].reshape(flat, width).astype(F32)
-        m["normed"] = (x * m["root_one"] * gain_one).astype(BF16)
-        packed = mm(m["normed"], attention_full)
-        m["q"], kv = split_heads(packed, m["cos"], m["sin"], q_heads, kv_heads, rows)
-        m["kv"] = earlier_gather(kv.reshape(trees, rows, -1), "context")
-    for m in state:
-        wide = attend_forward(ctx_ref, m["q"], m["kv"], m["ids"], q_heads, kv_heads, rows)
-        m["attended"] = mm(wide, select).astype(BF16)
-        product = mm_nt(m["attended"], o_full).reshape(trees, rows, width)
-        m["middle"] = m["x_here"] + line_reduce_scatter(product, share, "tensor")
-    for m in state:
-        middle = m["middle"]
+    def scattered(grad):
+        return lax.psum_scatter(grad, WEIGHT_AXES, scatter_dimension=0, tiled=True)
+
+    def together(name):
+        return jnp.concatenate([m[name].reshape(flat, -1) for m in state], axis=0)
+
+    def shaped(product):
+        return product.reshape(trees, rows, width)
+
+    stage = Stages()
+    a, b = state
+
+    def project(m):
+        def run(root):
+            x = m["x"].reshape(flat, width).astype(F32)
+            m["normed"] = (x * root * gain_one).astype(BF16)
+            packed = mm(m["normed"], attention_full)
+            m["q"], kv = split_heads(packed, m["cos"], m["sin"], q_heads, kv_heads, rows)
+            m["kv"] = EarlierGather(kv.reshape(trees, rows, -1), "context")
+            return (m["q"],)
+        return run
+
+    def attend(m):
+        def run(q):
+            m["kv_full"] = m["kv"].result()
+            wide = attend_forward(ctx_ref, q, m["kv_full"], m["ids"], q_heads, kv_heads, rows)
+            m["attended"] = mm(wide, select).astype(BF16)
+            product = mm_nt(m["attended"], o_full)
+            m["sum1"] = LineSum(shaped(product), share, "tensor")
+            return (product,)
+        return run
+
+    def mixed_back(m):
+        def run(dy):
+            m["dmixed"] = row_major(mm(dy.reshape(flat, width), down_full))
+            return (m["dmixed"],)
+        return run
+
+    def norm_two_of(m):
+        middle = m["x_here"] + m["sum1"].result()
         root = lax.rsqrt(jnp.mean(middle * middle, axis=-1, keepdims=True) + EPS)
-        m["root_two"] = root
-        m["normed_two"] = line_all_gather((middle * root * gain_two).astype(BF16), "tensor")
-
-    for m in state:
-        m["dmixed"] = mm(m["dy"].reshape(flat, width), down_full)
-    for m in state:
-        normed_two = m["normed_two"].reshape(flat, width)
-        gate = mm(normed_two, gate_full)
-        up = mm(normed_two, up_full)
-        sigmoid = 1.0 / (1.0 + jnp.exp(-gate))
-        silu = gate * sigmoid
-        m["mixed"] = (silu * up).astype(BF16)
-        slope = sigmoid * (1.0 + gate * (1.0 - sigmoid))
-        m["dgate"] = (m["dmixed"] * up * slope).astype(BF16)
-        m["dup"] = (m["dmixed"] * silu).astype(BF16)
-        dn2 = mm_nt(m["dgate"], gate_full) + mm_nt(m["dup"], up_full)
-        m["dn2"] = line_reduce_scatter(dn2.reshape(trees, rows, width), share, "tensor")
-    for m in state:
-        middle, dn2 = m["middle"], m["dn2"]
+        m["middle"], m["root_two"] = middle, root
+        m["gather1"] = LineGather((middle * root * gain_two).astype(BF16), "tensor")
+
+    def gate_of(m):
+        def run(normed_two):
+            m["normed_two"] = normed_two
+            m["gate"] = row_major(mm(normed_two, gate_full))
+            return (m["gate"],)
+        return run
+
+    def up_of(m):
+        def run(gate):
+            up = row_major(mm(m["normed_two"], up_full))
+            sigmoid = 1.0 / (1.0 + jnp.exp(-gate))
+            silu = gate * sigmoid
+            slope = sigmoid * (1.0 + gate * (1.0 - sigmoid))
+            m["mixed"] = row_major((silu * up).astype(BF16))
+            m["dgate"] = row_major((m["dmixed"] * up * slope).astype(BF16))
+            m["dup"] = row_major((m["dmixed"] * silu).astype(BF16))
+            return (m["mixed"], m["dgate"], m["dup"])
+        return run
+
+    def back_of(m):
+        def run(dgate):
+            product = mm_nt(dgate, gate_full) + mm_nt(m["dup"], up_full)
+            m["sum3"] = LineSum(shaped(product), share, "tensor")
+            return (product,)
+        return run
+
+    def norm_two_back(m):
+        middle, dn2 = m["middle"], m["sum3"].result()
         m["gain_two_grad"] = jnp.sum(dn2 * middle * m["root_two"], axis=(0, 1))
         m["dmiddle"] = m["dy_here"] + norm_back(dn2, middle, gain_two)
-        m["dmb"] = line_all_gather(m["dmiddle"].astype(BF16), "tensor").reshape(flat, width)
+        m["gather2"] = LineGather(m["dmiddle"].astype(BF16), "tensor")
+
+    def out_of(m):
+        def run(mixed):
+            product = mm_nt(mixed, down_full)
+            m["sum2"] = LineSum(shaped(product), share, "tensor")
+            return (product,)
+        return run
+
+    def attend_back(m):
+        def run(dmb):
+            m["dmb"] = dmb
+            dattended = mm(dmb, o_full).astype(BF16)
+            do_wide = mm_nt(dattended, select).astype(BF16)
+            m["dq"], dk, dv = attend_backward(
+                ctx_ref, m["q"], m["kv_full"], do_wide, m["ids"], q_heads, kv_heads, rows
+            )
+            m["dkv"] = EarlierReturn(jnp.concatenate([dk, dv], axis=2), "context")
+            return (m["dq"],)
+        return run
+
+    def norm_one_back(m):
+        def run(dq):
+            dkv = m["dkv"].result().reshape(flat, -1)
+            m["dqkv"] = pack_heads(
+                dq, dkv, m["cos"], m["sin"], q_heads, kv_heads, packed_width, rows
+            )
+            dn1 = mm_nt(m["dqkv"], attention_full)
+            x = m["x"].reshape(flat, width).astype(F32)
+            m["gain_one_grad"] = jnp.sum(dn1 * x * m["root_one"], axis=0)
+            m["sum4"] = LineSum(shaped(dn1), share, "tensor")
+            return (dn1,)
+        return run
+
+    weight_grads = {}
+
+    def weight_grad(name, left_of, right_of):
+        def run(tied):
+            left = tied if left_of is None else left_of()
+            weight_grads[name] = row_major(mm_tn(left, right_of()).astype(BF16))
+            return (weight_grads[name],)
+        return run
+
+    def both(*steps):
+        def run(*values):
+            return tuple(out for step, v in zip(steps, values) for out in step(v))
+        return run
+
+    stage([], project(a), [a["root_one"]])
+    stage([a["kv"]], project(b), [b["root_one"]])
+    stage([b["kv"]], attend(a), [a["q"]])
+    stage([a["sum1"]], attend(b), [b["q"]])
+    stage([a["sum1"], b["sum1"]])
+    stage([a["sum1"], b["sum1"]])
+    norm_two_of(a)
+    stage([a["gather1"], b["sum1"]], mixed_back(a), [a["dy"]])
+    norm_two_of(b)
+    stage([a["gather1"], b["gather1"]], mixed_back(b), [b["dy"]])
+    stage([a["gather1"], b["gather1"]])
+    stage([b["gather1"]], gate_of(a), [a["gather1"].result().reshape(flat, width)])
+    stage([], up_of(a), [a["gate"]])
+    stage([], back_of(a), [a["dgate"]])
+    stage([a["sum3"]], gate_of(b), [b["gather1"].result().reshape(flat, width)])
+    stage([a["sum3"]], up_of(b), [b["gate"]])
+    dy_all = cotangent.reshape(-1, width)
+    stage(
+        [a["sum3"]],
+        both(back_of(b), weight_grad("down", lambda: dy_all, lambda: together("mixed"))),
+        [b["dgate"], b["mixed"]],
+    )
+    down_grad = scattered(weight_grads["down"])
+    norm_two_back(a)
+    normed_two_all = together("normed_two")
+    stage(
+        [a["gather2"], b["sum3"]],
+        weight_grad("gate", None, lambda: together("dgate")),
+        [normed_two_all],
+    )
+    gate_grad = scattered(weight_grads["gate"])
+    stage(
+        [a["gather2"], b["sum3"]],
+        weight_grad("up", None, lambda: together("dup")),
+        [normed_two_all],
+    )
+    up_grad = scattered(weight_grads["up"])
+    stage([a["gather2"], b["sum3"]], both(out_of(a), out_of(b)), [a["mixed"], b["mixed"]])
+    norm_two_back(b)
+    stage.wait_for(down_grad)
+    stage([b["gather2"]], attend_back(a), [a["gather2"].result().reshape(flat, width)])
+    stage([b["gather2"], a["dkv"]])
+    stage([b["gather2"], a["sum2"]], norm_one_back(a), [a["dq"]])
+    stage.wait_for(gate_grad)
+    stage(
+        [a["sum4"], a["sum2"]], attend_back(b), [b["gather2"].result().reshape(flat, width)]
+    )
+    stage(
+        [a["sum4"], b["dkv"], b["sum2"]],
+        weight_grad("o", None, lambda: together("attended")),
+        [together("dmb")],
+    )
+    o_grad = scattered(weight_grads["o"])
+    stage([a["sum4"], a["sum2"]], norm_one_back(b), [b["dq"]])
+
+    def attention_weight_grad():
+        grad = mm_tn(together("normed"), together("dqkv"))
+        gains = [sum(m[name] for m in state) for name in ("gain_one_grad", "gain_two_grad")]
+        columns = lax.broadcasted_iota(jnp.int32, grad.shape, 1)
+        grad = jnp.where(
+            columns == used,
+            gains[0][:, None],
+            jnp.where(columns == used + 1, gains[1][:, None], grad),
+        )
+        weight_grads["attention"] = grad.astype(BF16)
+        return (weight_grads["attention"],)
+
+    stage.wait_for(up_grad)
+    stage([b["sum4"], b["sum2"]], attention_weight_grad)
+    attention_grad = scattered(weight_grads["attention"]).astype(F32)
+    stage([b["sum4"], b["sum2"]])
+    stage.wait_for(o_grad)
+    stage([b["sum4"]])
     for m in state:
-        out = mm_nt(m["mixed"], down_full).reshape(trees, rows, width)
-        m["out"] = (m["middle"] + line_reduce_scatter(out, share, "tensor")).astype(BF16)
-
-    def together(name):
-        return jnp.concatenate([m[name].reshape(flat, -1) for m in state], axis=0)
-
-    def scattered(grad):
-        return lax.psum_scatter(grad.astype(BF16), WEIGHT_AXES, scatter_dimension=0, tiled=True)
-
-    dy_all = cotangent.reshape(-1, width)
-    normed_two_all = together("normed_two")
-    down_grad = scattered(mm_tn(dy_all, together("mixed")))
-    gate_grad = scattered(mm_tn(normed_two_all, together("dgate")))
-    up_grad = scattered(mm_tn(normed_two_all, together("dup")))
-
-    for m in state:
-        dattended = mm(m["dmb"], o_full).astype(BF16)
-        do_wide = mm_nt(dattended, select).astype(BF16)
-        dq, dk, dv = attend_backward(
-            ctx_ref, m["q"], m["kv"], do_wide, m["ids"], q_heads, kv_heads, rows
-        )
-        dkv = earlier_return(jnp.concatenate([dk, dv], axis=2), "context").reshape(flat, -1)
-        m["dqkv"] = pack_heads(
-            dq, dkv, m["cos"], m["sin"], q_heads, kv_heads, packed_width, rows
-        )
-        dn1 = mm_nt(m["dqkv"], attention_full)
-        x = m["x"].reshape(flat, width).astype(F32)
-        m["gain_one_grad"] = jnp.sum(dn1 * x * m["root_one"], axis=0)
-        m["dn1"] = line_reduce_scatter(dn1.reshape(trees, rows, width), share, "tensor")
-    o_grad = scattered(mm_tn(together("dmb"), together("attended")))
-    for m in state:
-        m["dx"] = (m["dmiddle"] + norm_back(m["dn1"], m["x_here"], gain_one)).astype(BF16)
-
-    attention_grad = mm_tn(together("normed"), together("dqkv"))
-    gains = [sum(m[name] for m in state) for name in ("gain_one_grad", "gain_two_grad")]
-    columns = lax.broadcasted_iota(jnp.int32, attention_grad.shape, 1)
-    attention_grad = jnp.where(
-        columns == used,
-        gains[0][:, None],
-        jnp.where(columns == used + 1, gains[1][:, None], attention_grad),
-    )
-    attention_grad = scattered(attention_grad).astype(F32)
+        m["out"] = (m["middle"] + m["sum2"].result()).astype(BF16)
+        m["dx"] = (m["dmiddle"] + norm_back(m["sum4"].result(), m["x_here"], gain_one)).astype(BF16)
+
     gain_grads = small_sum(attention_grad[:, used : used + 2], "tensor")
     return (
         jnp.concatenate([m["out"] for m in state], axis=0),

time: 1270 us -> 895 us (0.70)
  waiting for transfers between devices: 620 us -> 191 us
  other arithmetic: 57.3 us -> 113 us
  matrix products: 239 us -> 226 us
    ppermute x76, waiting for transfers between devices: 436 us -> 157 us  [__call__(): results.append(lax.ppermute(tied[at], axis, pairs))]
    reduce_scatter x4 -> x5, waiting for transfers between devices: 124 us -> 0.01 us  [scattered(): return lax.psum_scatter(grad, WEIGHT_AXES, scatter_dimension=0, tiled=True)]
    convert_element_type x28 -> x24, other arithmetic: 15.9 us -> 46.8 us  [the longest x16 30.1 us: sends(): found.append((value.astype(BF16), self.axis, pairs))]
    dot_general x10, matrix products: 88.9 us -> 70.5 us  [mm(): lax.dot_general(left, right, (((1,), (0,)), ((), ())), preferred_element_...]
    all_gather x1, waiting for transfers between devices: 17.9 us -> 0.02 us  [on_device(): gate_full = lax.all_gather(gate_weight, WEIGHT_AXES, axis=0, tiled=True)]
    dynamic_update_slice x16, other arithmetic: 12 us -> 28.7 us  [the longest x12 21.2 us: result(): result = lax.dynamic_update_slice_in_dim(result, value, slot * size, 1)]
    dot_general x12, matrix products: 88.9 us -> 103 us  [mm_nt(): lax.dot_general(left, right, (((1,), (1,)), ((), ())), preferred_element_...]
    unnamed x105 -> x223, local copies, waits for them, and re-layouts: 33.1 us -> 21.8 us
  transfers between devices with their start and end apart: 89 -> 89, of which waited for: 50 -> 24; matrix products, arithmetic and copies ran while one was open for 17% -> 38% of each run, Pallas kernels for 3% -> 9%
where the time goes in v2:
time: 895 us; the launch traced here: 881 us
  matrix products  226 us (25%)
  starting transfers between devices  192 us (21%)
  waiting for transfers between devices  191 us (21%)
  other arithmetic  113 us (13%)
  Pallas kernels  80.9 us (9%)
  local copies, waits for them, and re-layouts  61.6 us (7%)
  between operations  16.8 us (2%)
    ppermute x76, starting transfers between devices, __call__(): results.append(lax.ppermute(tied[at], axis, pairs))  188 us
    ppermute x76, waiting for transfers between devices, __call__(): results.append(lax.ppermute(tied[at], axis, pairs))  157 us
    dot_general x12, matrix products, mm_nt(): lax.dot_general(left, right, (((1,), (1,)), ((), ())), preferred_element_...  103 us
    dot_general x10, matrix products, mm(): lax.dot_general(left, right, (((1,), (0,)), ((), ())), preferred_element_...  70.5 us
    dot_general x5, matrix products, mm_tn(): lax.dot_general(left, right, (((0,), (0,)), ((), ())), preferred_element_...  52.4 us
    pallas_call x2, Pallas kernels, attend_backward(): pl.pallas_call(functools.partial(backward_kernel, rows, tree_len, block,...  36 us
    convert_element_type x16, other arithmetic, sends(): found.append((value.astype(BF16), self.axis, pairs))  30.1 us
    all_gather x1, waiting for transfers between devices, on_device(): lax.all_gather(attention_block, WEIGHT_AXES, axis=0, tiled=True)  27.7 us
  transfers between devices with their start and end apart: 89, of which 24 were waited for; matrix products, arithmetic and copies ran while one was open for 38% of the time, Pallas kernels for 9%

profile of v2, /device:TPU:0, one launch (start us, length us, event | category | flops | bytes accessed | tf_op | source)
XLA Modules:
  0.0 881.5 jit_solution(1750614581529296805)
XLA Ops:
  29.1 27.7 %all-gather.6.cloned.1.call-done = bf16[2560,1024]{1,0:T(8,128)(2,1)} async-done(((bf16[320,1024]{1,0:T(8,128)(2,1)}), bf16[2560,1024]{1,0:T(8,128)(2,1)}) %all-gather.6.cloned.1.call-update) | async-done | bytes 5242896 | tf_op jit(solution)/shard_map/all_gather | solution.py:476
  101.9 12.7 %attend_forward.2 = bf16[512,1024]{1,0:T(8,128)(2,1)} custom-call(s32[1]{0:T(128)} %bitcast.ctx_ref, bf16[512,1024]{1,0:T(8,128)(2,1)} %get-tuple-element.123.q_ref, bf16[1,1024,512]{2,1,0:T(8,128)(2,1)} %copy-done.43, bf16[1,1024,512]{2,1,0:T(8,128)(2,1)} %copy-done.43, s32[1,512,1]{2,1,0:T(8,128)} %copy.54.seg_q, s32[1,512,1]{2,1,0:T(8,128)} %copy.55.par_q, ...), custom_call_target="tpu_custom_call" | custom-call | flops 2147483648 | bytes 4194304 | tf_op jit(solution)/shard_map/attend_forward/pallas_call | solution.py:242
  131.8 12.6 %attend_forward.3 = bf16[512,1024]{1,0:T(8,128)(2,1)} custom-call(s32[1]{0:T(128)} %bitcast.ctx_ref, bf16[512,1024]{1,0:T(8,128)(2,1)} %get-tuple-element.127.q_ref, bf16[1,1024,512]{2,1,0:T(8,128)(2,1)} %copy-done.44, bf16[1,1024,512]{2,1,0:T(8,128)(2,1)} %copy-done.44, s32[1,512,1]{2,1,0:T(8,128)} %copy.57.seg_q, s32[1,512,1]{2,1,0:T(8,128)} %copy.58.par_q, ...), custom_call_target="tpu_custom_call" | custom-call | flops 2147483648 | bytes 4194304 | tf_op jit(solution)/shard_map/attend_forward/pallas_call | solution.py:242
  159.7 10.7 %collective-permute-done.6 = bf16[1,128,2560]{2,1,0:T(8,128)(2,1)S(1)} collective-permute-done((bf16[1,128,2560]{2,1,0:T(8,128)(2,1)S(1)}, bf16[1,128,2560]{2,1,0:T(8,128)(2,1)S(1)}, u32[]{:S(2)}, u32[]{:S(2)}) %collective-permute-start.6) | collective-permute-done | bytes 655392 | tf_op jit(solution)/shard_map/ppermute | solution.py:422
  172.9 8.6 collective-permute-done.4
  202.7 9.0 %collective-permute-done.10 = bf16[1,128,2560]{2,1,0:T(8,128)(2,1)S(1)} collective-permute-done((bf16[1,128,2560]{2,1,0:T(8,128)(2,1)S(1)}, bf16[1,128,2560]{2,1,0:T(8,128)(2,1)S(1)}, u32[]{:S(2)}, u32[]{:S(2)}) %collective-permute-start.10) | collective-permute-done | bytes 655392 | tf_op jit(solution)/shard_map/ppermute | solution.py:422
  243.0 11.2 %fusion.27 = f32[512,1728]{1,0:T(8,128)} fusion(bf16[2560,1728]{1,0:T(8,128)(2,1)} %all-gather.10.cloned.1.call-done, bf16[1,512,2560]{2,1,0:T(8,128)(2,1)} %get-tuple-element.136), kind=kOutput, calls=%fused_computation.49 | convolution fusion | flops 4529848320 | bytes 15007744 | tf_op jit(solution)/shard_map/dot_general | solution.py:36
  270.4 13.1 %collective-permute-done.19 = bf16[1,128,2560]{2,1,0:T(8,128)(2,1)S(1)} collective-permute-done((bf16[1,128,2560]{2,1,0:T(8,128)(2,1)}, bf16[1,128,2560]{2,1,0:T(8,128)(2,1)S(1)}, u32[]{:S(2)}, u32[]{:S(2)}) %collective-permute-start.19) | collective-permute-done | bytes 655392 | tf_op jit(solution)/shard_map/ppermute | solution.py:422
  288.4 10.1 %collective-permute-done.22 = bf16[1,128,2560]{2,1,0:T(8,128)(2,1)} collective-permute-done((bf16[1,128,2560]{2,1,0:T(8,128)(2,1)}, bf16[1,128,2560]{2,1,0:T(8,128)(2,1)}, u32[]{:S(2)}, u32[]{:S(2)}) %collective-permute-start.22) | collective-permute-done | bytes 655392 | tf_op jit(solution)/shard_map/ppermute | solution.py:422
  303.7 8.0 collective-permute-done.21
  314.0 11.1 %fusion.135 = f32[512,1728]{1,0:T(8,128)} fusion(bf16[512,2560]{1,0:T(8,128)(2,1)} %bitcast_dynamic-update-slice_fusion.12, bf16[2560,1728]{1,0:T(8,128)(2,1)} %all-gather.14.cloned.1.call-done), kind=kOutput, calls=%fused_computation.309 | convolution fusion | flops 4529848320 | bytes 15007744 | tf_op jit(solution)/shard_map/dot_general | solution.py:36
  325.1 9.0 %fusion.134 = f32[512,1728]{1,0:T(8,128)S(1)} fusion(bf16[512,2560]{1,0:T(8,128)(2,1)} %bitcast_dynamic-update-slice_fusion.12, bf16[2560,1728]{1,0:T(8,128)(2,1)} %all-gather.12.cloned.1.call-done), kind=kOutput, calls=%fused_computation.308 | convolution fusion | flops 4529848320 | bytes 15007744 | tf_op jit(solution)/shard_map/dot_general | solution.py:36
  344.8 9.6 %convolution_add_fusion.1 = f32[512,2560]{1,0:T(8,128)S(1)} fusion(f32[512,2560]{1,0:T(8,128)} %fusion.136, bf16[512,1728]{1,0:T(8,128)(2,1)S(1)} %get-tuple-element.291, bf16[2560,1728]{1,0:T(8,128)(2,1)} %all-gather.12.cloned.1.call-done), kind=kOutput, calls=%fused_computation.27 | convolution fusion | flops 4531159040 | bytes 21102592 | tf_op jit(solution)/shard_map/dot_general | solution.py:40
  367.0 8.9 %fusion.138 = f32[512,1728]{1,0:T(8,128)S(1)} fusion(bf16[512,2560]{1,0:T(8,128)(2,1)} %bitcast_dynamic-update-slice_fusion.8, bf16[2560,1728]{1,0:T(8,128)(2,1)} %all-gather.12.cloned.1.call-done), kind=kOutput, calls=%fused_computation.312 | convolution fusion | flops 4529848320 | bytes 15007744 | tf_op jit(solution)/shard_map/dot_general | solution.py:36
  389.7 12.3 %fusion = bf16[2560,1728]{1,0:T(8,128)(2,1)} fusion(bf16[1024,2560]{1,0:T(8,128)(2,1)S(1)} %bitcast.378, bf16[512,1728]{1,0:T(8,128)(2,1)S(1)} %get-tuple-element.179, bf16[512,1728]{1,0:T(8,128)(2,1)S(1)} %get-tuple-element.174), kind=kOutput, calls=%fused_computation.4 | convolution fusion | flops 9071198208 | bytes 17629184 | tf_op jit(solution)/shard_map/dot_general | solution.py:44
  410.4 11.2 %fusion.139 = f32[512,2560]{1,0:T(8,128)} fusion(bf16[512,1728]{1,0:T(8,128)(2,1)S(1)} %copy-done.30, bf16[2560,1728]{1,0:T(8,128)(2,1)} %all-gather.12.cloned.1.call-done), kind=kOutput, calls=%fused_computation.313 | convolution fusion | flops 4529848320 | bytes 15859712 | tf_op jit(solution)/shard_map/dot_general | solution.py:40
  432.8 9.9 %convolution_add_fusion = f32[512,2560]{1,0:T(8,128)S(1)} fusion(f32[512,2560]{1,0:T(8,128)} %fusion.139, bf16[512,1728]{1,0:T(8,128)(2,1)S(1)} %copy-done.34, bf16[2560,1728]{1,0:T(8,128)(2,1)} %all-gather.14.cloned.1.call-done), kind=kOutput, calls=%fused_computation.26 | convolution fusion | flops 4531159040 | bytes 21102592 | tf_op jit(solution)/shard_map/dot_general | solution.py:40
  452.1 12.0 %convolution_convert_fusion.1 = bf16[2560,1728]{1,0:T(8,128)(2,1)} fusion(bf16[1024,2560]{1,0:T(8,128)(2,1)S(1)} %copy-done.37, bf16[512,1728]{1,0:T(8,128)(2,1)S(1)} %copy-done.35, bf16[512,1728]{1,0:T(8,128)(2,1)S(1)} %copy-done.33), kind=kOutput, calls=%fused_computation.1 | convolution fusion | flops 9071198208 | bytes 17629184 | tf_op jit(solution)/shard_map/dot_general | solution.py:44
  472.1 8.6 collective-permute-done.34
  493.6 8.8 collective-permute-start.38
  504.1 13.9 %convolution_convert_fusion = bf16[2560,1728]{1,0:T(8,128)(2,1)} fusion(bf16[1024,2560]{1,0:T(8,128)(2,1)} %copy-done.36, bf16[512,1728]{1,0:T(8,128)(2,1)S(1)} %copy-done.31, bf16[512,1728]{1,0:T(8,128)(2,1)S(1)} %copy-done.27), kind=kOutput, calls=%fused_computation | convolution fusion | flops 9071198208 | bytes 17629184 | tf_op jit(solution)/shard_map/dot_general | solution.py:44
  532.1 10.3 %fusion.140 = f32[512,2560]{1,0:T(8,128)} fusion(bf16[512,1728]{1,0:T(8,128)(2,1)S(1)} %get-tuple-element.174, bf16[2560,1728]{1,0:T(8,128)(2,1)} %all-gather.10.cloned.1.call-done), kind=kOutput, calls=%fused_computation.314 | convolution fusion | flops 4529848320 | bytes 15859712 | tf_op jit(solution)/shard_map/dot_general | solution.py:40
  542.4 10.8 %fusion.141 = f32[512,2560]{1,0:T(8,128)} fusion(bf16[512,1728]{1,0:T(8,128)(2,1)S(1)} %copy-done.29, bf16[2560,1728]{1,0:T(8,128)(2,1)} %all-gather.10.cloned.1.call-done), kind=kOutput, calls=%fused_computation.315 | convolution fusion | flops 4529848320 | bytes 15859712 | tf_op jit(solution)/shard_map/dot_general | solution.py:40
  571.6 9.5 %convolution_convert_fusion.5.do_ref = bf16[512,1024]{1,0:T(8,128)(2,1)} fusion(bf16[1024,640]{1,0:T(8,128)(2,1)} %constant.100.clone, bf16[512,2560]{1,0:T(8,128)(2,1)} %bitcast_dynamic-update-slice_fusion.4, bf16[2560,640]{1,0:T(8,128)(2,1)} %all-gather.8.cloned.1.call-done), kind=kOutput, calls=%fused_computation.64 | convolution fusion | flops 2349662208 | bytes 8257536 | tf_op jit(solution)/shard_map/dot_general | solution.py:40
  581.1 18.0 %attend_backward.2 = (bf16[512,1024]{1,0:T(8,128)(2,1)}, f32[1,1024,256]{2,1,0:T(8,128)}, f32[1,1024,256]{2,1,0:T(8,128)}) custom-call(s32[1]{0:T(128)} %bitcast.ctx_ref, bf16[512,1024]{1,0:T(8,128)(2,1)} %get-tuple-element.123.q_ref, bf16[1,1024,512]{2,1,0:T(8,128)(2,1)} %copy-done.43, bf16[1,1024,512]{2,1,0:T(8,128)(2,1)} %copy-done.43, ...), custom_call_target="tpu_custom_call" | custom-call | flops 5368709120 | bytes 6291456 | tf_op jit(solution)/shard_map/attend_backward/pallas_call | solution.py:267
  610.8 12.6 %collective-permute-done.48 = bf16[1,512,512]{2,1,0:T(8,128)(2,1)S(1)} collective-permute-done((bf16[1,512,512]{2,1,0:T(8,128)(2,1)S(1)}, bf16[1,512,512]{2,1,0:T(8,128)(2,1)S(1)}, u32[]{:S(2)}, u32[]{:S(2)}) %collective-permute-start.48) | collective-permute-done | bytes 524320 | tf_op jit(solution)/shard_map/ppermute | solution.py:422
  665.2 8.4 convolution_convert_fusion.4.do_ref
  673.6 17.9 %attend_backward.3 = (bf16[512,1024]{1,0:T(8,128)(2,1)}, f32[1,1024,256]{2,1,0:T(8,128)}, f32[1,1024,256]{2,1,0:T(8,128)}) custom-call(s32[1]{0:T(128)} %bitcast.ctx_ref, bf16[512,1024]{1,0:T(8,128)(2,1)} %get-tuple-element.127.q_ref, bf16[1,1024,512]{2,1,0:T(8,128)(2,1)} %copy-done.44, bf16[1,1024,512]{2,1,0:T(8,128)(2,1)} %copy-done.44, ...), custom_call_target="tpu_custom_call" | custom-call | flops 5368709120 | bytes 6291456 | tf_op jit(solution)/shard_map/attend_backward/pallas_call | solution.py:267
  754.1 12.1 %fusion.10 = (f32[2560]{0:T(1024)S(1)}, f32[2560]{0:T(1024)S(1)}, f32[512,2560]{1,0:T(8,128)}) fusion(f32[512]{0:T(512)S(1)} %copy-done.71, bf16[2,512,2560]{2,1,0:T(8,128)(2,1)} %param.15, f32[512]{0:T(512)S(1)} %copy-done.73, f32[512,2560]{1,0:T(8,128)} %copy-done.4, bf16[512,1024]{1,0:T(8,128)(2,1)} %pack_heads.3, ...), kind=kOutput, calls=%fused_computation.20 | convolution fusion | flops 2694835200 | bytes 22044672 | tf_op jit(solution)/shard_map/dot_general | solution.py:40
  766.3 8.3 select_convert_fusion
  788.8 9.8 %collective-permute-done.66 = bf16[1,128,2560]{2,1,0:T(8,128)(2,1)S(1)} collective-permute-done((bf16[1,128,2560]{2,1,0:T(8,128)(2,1)S(1)}, bf16[1,128,2560]{2,1,0:T(8,128)(2,1)S(1)}, u32[]{:S(2)}, u32[]{:S(2)}) %collective-permute-start.66) | collective-permute-done | bytes 655392 | tf_op jit(solution)/shard_map/ppermute | solution.py:422
  845.9 8.8 collective-permute-done.75
  (544 shorter events, 498.9 us)
Async XLA Ops:
  7.2 49.6 %all-gather.6.cloned.1.call-start = ((), (), s32[]{:S(2)}) async-start(), calls=%async_computation.5 | async-start | bytes 5898240 | tf_op jit(solution)/shard_map/all_gather | solution.py:476
  12.9 103.9 %all-gather.8.cloned.1.call-start = ((), (), s32[]{:S(2)}) async-start(), calls=%async_computation.6 | async-start | bytes 3686400 | tf_op jit(solution)/shard_map/all_gather | solution.py:477
  13.6 229.3 %all-gather.10.cloned.1.call-start = ((), (), s32[]{:S(2)}) async-start(), calls=%async_computation.7 | async-start | bytes 10321920 | tf_op jit(solution)/shard_map/all_gather | solution.py:478
  14.4 299.6 %all-gather.14.cloned.1.call-start = ((), (), s32[]{:S(2)}) async-start(), calls=%async_computation.9 | async-start | bytes 10321920 | tf_op jit(solution)/shard_map/all_gather | solution.py:479
  14.9 310.2 %all-gather.12.cloned.1.call-start = ((), (), s32[]{:S(2)}) async-start(), calls=%async_computation.8 | async-start | bytes 10321920 | tf_op jit(solution)/shard_map/all_gather | solution.py:480
  15.5 548.4 %reduce-scatter.6.cloned.1.call-start = ((), (), s32[]{:S(2)}) async-start(), calls=%async_computation.10 | async-start | bytes 10321920 | tf_op jit(solution)/shard_map/reduce_scatter | solution.py:521
  95.7 27.9 %collective-permute-start.1 = (bf16[1,512,512]{2,1,0:T(8,128)(2,1)}, bf16[1,512,512]{2,1,0:T(8,128)(2,1)}, u32[]{:S(2)}, u32[]{:S(2)}) collective-permute-start(bf16[1,512,512]{2,1,0:T(8,128)(2,1)} %bitcast.12), channel_id=1, source_target_pairs={{0,4},{1,5},{2,6},{3,7},{8,12},{9,13},{10,14},{11,15},{16,20},{17,... | collective-permute-start | bytes 1572872 | tf_op jit(solution)/shard_map/ppermute | solution.py:422
  123.7 28.6 %collective-permute-start.2 = (bf16[1,128,2560]{2,1,0:T(8,128)(2,1)S(1)}, bf16[1,128,2560]{2,1,0:T(8,128)(2,1)}, u32[]{:S(2)}, u32[]{:S(2)}) collective-permute-start(bf16[1,128,2560]{2,1,0:T(8,128)(2,1)S(1)} %get-tuple-element.125), channel_id=1, source_target_pairs={{0,1},{4,5},{8,9},{12,13},{16,17},{20,21},{24,25},{28,29}} | collective-permute-start | bytes 1966088 | tf_op jit(solution)/shard_map/ppermute | solution.py:422
  127.7 24.6 %collective-permute-start.3 = (bf16[1,128,2560]{2,1,0:T(8,128)(2,1)S(1)}, bf16[1,128,2560]{2,1,0:T(8,128)(2,1)}, u32[]{:S(2)}, u32[]{:S(2)}) collective-permute-start(bf16[1,128,2560]{2,1,0:T(8,128)(2,1)S(1)} %get-tuple-element.126), channel_id=1, source_target_pairs={{3,2},{7,6},{11,10},{15,14},{19,18},{23,22},{27,26},{31,30}} | collective-permute-start | bytes 1966088 | tf_op jit(solution)/shard_map/ppermute | solution.py:422
  220.6 33.5 %collective-permute-start.12 = (bf16[1,128,2560]{2,1,0:T(8,128)(2,1)S(1)}, bf16[1,128,2560]{2,1,0:T(8,128)(2,1)}, u32[]{:S(2)}, u32[]{:S(2)}) collective-permute-start(bf16[1,128,2560]{2,1,0:T(8,128)(2,1)S(1)} %get-tuple-element.138), channel_id=1, source_target_pairs={{0,1},{1,2},{2,3},{4,5},{5,6},{6,7},{8,9},{9,10},{10,11},{12,13},{... | collective-permute-start | bytes 1966088 | tf_op jit(solution)/shard_map/ppermute | solution.py:422
  226.1 28.1 %collective-permute-start.13 = (bf16[1,128,2560]{2,1,0:T(8,128)(2,1)S(1)}, bf16[1,128,2560]{2,1,0:T(8,128)(2,1)S(1)}, u32[]{:S(2)}, u32[]{:S(2)}) collective-permute-start(bf16[1,128,2560]{2,1,0:T(8,128)(2,1)S(1)} %get-tuple-element.138), channel_id=1, source_target_pairs={{3,2},{2,1},{1,0},{7,6},{6,5},{5,4},{11,10},{10,9},{9,8},{15,14},{... | collective-permute-start | bytes 1966088 | tf_op jit(solution)/shard_map/ppermute | solution.py:422
  286.4 25.4 %collective-permute-start.21 = (bf16[1,128,2560]{2,1,0:T(8,128)(2,1)S(1)}, bf16[1,128,2560]{2,1,0:T(8,128)(2,1)}, u32[]{:S(2)}, u32[]{:S(2)}) collective-permute-start(bf16[1,128,2560]{2,1,0:T(8,128)(2,1)S(1)} %collective-permute-done.19), channel_id=1, source_target_pairs={{2,1},{1,0},{6,5},{5,4},{10,9},{9,8},{14,13},{13,12},{18,17},{17,1... | collective-permute-start | bytes 1966088 | tf_op jit(solution)/shard_map/ppermute | solution.py:422
  402.0 251.7 %reduce-scatter.8.cloned.1.call-start = ((), (), s32[]{:S(2)}) async-start(), calls=%async_computation.11 | async-start | bytes 10321920 | tf_op jit(solution)/shard_map/reduce_scatter | solution.py:521
  464.2 248.0 %reduce-scatter.10.cloned.1.call-start = ((), (), s32[]{:S(2)}) async-start(), calls=%async_computation.12 | async-start | bytes 10321920 | tf_op jit(solution)/shard_map/reduce_scatter | solution.py:521
  490.8 30.0 %collective-permute-start.36 = (bf16[1,128,2560]{2,1,0:T(8,128)(2,1)S(1)}, bf16[1,128,2560]{2,1,0:T(8,128)(2,1)}, u32[]{:S(2)}, u32[]{:S(2)}) collective-permute-start(bf16[1,128,2560]{2,1,0:T(8,128)(2,1)S(1)} %collective-permute-done.32), channel_id=1, source_target_pairs={{1,2},{2,3},{5,6},{6,7},{9,10},{10,11},{13,14},{14,15},{17,18},{18... | collective-permute-start | bytes 1966088 | tf_op jit(solution)/shard_map/ppermute | solution.py:422
  492.3 28.5 %collective-permute-start.37 = (bf16[1,128,2560]{2,1,0:T(8,128)(2,1)S(1)}, bf16[1,128,2560]{2,1,0:T(8,128)(2,1)}, u32[]{:S(2)}, u32[]{:S(2)}) collective-permute-start(bf16[1,128,2560]{2,1,0:T(8,128)(2,1)S(1)} %collective-permute-done.33), channel_id=1, source_target_pairs={{2,1},{1,0},{6,5},{5,4},{10,9},{9,8},{14,13},{13,12},{18,17},{17,1... | collective-permute-start | bytes 1966088 | tf_op jit(solution)/shard_map/ppermute | solution.py:422
  518.1 314.8 %reduce-scatter.12.cloned.1.call-start = ((), (), s32[]{:S(2)}) async-start(), calls=%async_computation.13 | async-start | bytes 3686400 | tf_op jit(solution)/shard_map/reduce_scatter | solution.py:521
  520.9 32.4 %collective-permute-start.40 = (bf16[1,128,2560]{2,1,0:T(8,128)(2,1)S(1)}, bf16[1,128,2560]{2,1,0:T(8,128)(2,1)S(1)}, u32[]{:S(2)}, u32[]{:S(2)}) collective-permute-start(bf16[1,128,2560]{2,1,0:T(8,128)(2,1)S(1)} %get-tuple-element.175), channel_id=1, source_target_pairs={{0,1},{1,2},{2,3},{4,5},{5,6},{6,7},{8,9},{9,10},{10,11},{12,13},{... | collective-permute-start | bytes 1966088 | tf_op jit(solution)/shard_map/ppermute | solution.py:422
  530.1 25.2 %collective-permute-start.42 = (bf16[1,128,2560]{2,1,0:T(8,128)(2,1)}, bf16[1,128,2560]{2,1,0:T(8,128)(2,1)S(1)}, u32[]{:S(2)}, u32[]{:S(2)}) collective-permute-start(bf16[1,128,2560]{2,1,0:T(8,128)(2,1)} %collective-permute-done.37), channel_id=1, source_target_pairs={{1,0},{5,4},{9,8},{13,12},{17,16},{21,20},{25,24},{29,28}} | collective-permute-start | bytes 1966088 | tf_op jit(solution)/shard_map/ppermute | solution.py:422
  531.4 27.0 %collective-permute-start.43 = (bf16[1,128,2560]{2,1,0:T(8,128)(2,1)}, bf16[1,128,2560]{2,1,0:T(8,128)(2,1)S(1)}, u32[]{:S(2)}, u32[]{:S(2)}) collective-permute-start(bf16[1,128,2560]{2,1,0:T(8,128)(2,1)} %collective-permute-done.36), channel_id=1, source_target_pairs={{2,3},{6,7},{10,11},{14,15},{18,19},{22,23},{26,27},{30,31}} | collective-permute-start | bytes 1966088 | tf_op jit(solution)/shard_map/ppermute | solution.py:422
  563.9 36.9 %collective-permute-start.44 = (bf16[1,128,2560]{2,1,0:T(8,128)(2,1)}, bf16[1,128,2560]{2,1,0:T(8,128)(2,1)}, u32[]{:S(2)}, u32[]{:S(2)}) collective-permute-start(bf16[1,128,2560]{2,1,0:T(8,128)(2,1)} %get-tuple-element.181), channel_id=1, source_target_pairs={{0,1},{1,2},{2,3},{4,5},{5,6},{6,7},{8,9},{9,10},{10,11},{12,13},{... | collective-permute-start | bytes 1966088 | tf_op jit(solution)/shard_map/ppermute | solution.py:422
  569.9 31.0 %collective-permute-start.45 = (bf16[1,128,2560]{2,1,0:T(8,128)(2,1)}, bf16[1,128,2560]{2,1,0:T(8,128)(2,1)S(1)}, u32[]{:S(2)}, u32[]{:S(2)}) collective-permute-start(bf16[1,128,2560]{2,1,0:T(8,128)(2,1)} %get-tuple-element.181), channel_id=1, source_target_pairs={{3,2},{2,1},{1,0},{7,6},{6,5},{5,4},{11,10},{10,9},{9,8},{15,14},{... | collective-permute-start | bytes 1966088 | tf_op jit(solution)/shard_map/ppermute | solution.py:422
  624.6 25.6 %collective-permute-start.49 = (bf16[1,128,2560]{2,1,0:T(8,128)(2,1)}, bf16[1,128,2560]{2,1,0:T(8,128)(2,1)}, u32[]{:S(2)}, u32[]{:S(2)}) collective-permute-start(bf16[1,128,2560]{2,1,0:T(8,128)(2,1)} %get-tuple-element.190), channel_id=1, source_target_pairs={{0,1},{4,5},{8,9},{12,13},{16,17},{20,21},{24,25},{28,29}} | collective-permute-start | bytes 1966088 | tf_op jit(solution)/shard_map/ppermute | solution.py:422
  653.7 45.3 %collective-permute-start.53 = (bf16[1,128,2560]{2,1,0:T(8,128)(2,1)}, bf16[1,128,2560]{2,1,0:T(8,128)(2,1)}, u32[]{:S(2)}, u32[]{:S(2)}) collective-permute-start(bf16[1,128,2560]{2,1,0:T(8,128)(2,1)} %get-tuple-element.194), channel_id=1, source_target_pairs={{0,1},{4,5},{8,9},{12,13},{16,17},{20,21},{24,25},{28,29}} | collective-permute-start | bytes 1966088 | tf_op jit(solution)/shard_map/ppermute | solution.py:422
  659.9 39.1 %collective-permute-start.54 = (bf16[1,128,2560]{2,1,0:T(8,128)(2,1)S(1)}, bf16[1,128,2560]{2,1,0:T(8,128)(2,1)}, u32[]{:S(2)}, u32[]{:S(2)}) collective-permute-start(bf16[1,128,2560]{2,1,0:T(8,128)(2,1)S(1)} %copy-done.57), channel_id=1, source_target_pairs={{3,2},{7,6},{11,10},{15,14},{19,18},{23,22},{27,26},{31,30}} | collective-permute-start | bytes 1966088 | tf_op jit(solution)/shard_map/ppermute | solution.py:422
  661.4 40.4 %collective-permute-start.55 = (bf16[1,128,2560]{2,1,0:T(8,128)(2,1)}, bf16[1,128,2560]{2,1,0:T(8,128)(2,1)}, u32[]{:S(2)}, u32[]{:S(2)}) collective-permute-start(bf16[1,128,2560]{2,1,0:T(8,128)(2,1)} %get-tuple-element.199), channel_id=1, source_target_pairs={{0,1},{1,2},{4,5},{5,6},{8,9},{9,10},{12,13},{13,14},{16,17},{17,1... | collective-permute-start | bytes 1966088 | tf_op jit(solution)/shard_map/ppermute | solution.py:422
  663.6 38.3 %collective-permute-start.56 = (bf16[1,128,2560]{2,1,0:T(8,128)(2,1)}, bf16[1,128,2560]{2,1,0:T(8,128)(2,1)}, u32[]{:S(2)}, u32[]{:S(2)}) collective-permute-start(bf16[1,128,2560]{2,1,0:T(8,128)(2,1)} %get-tuple-element.200), channel_id=1, source_target_pairs={{3,2},{2,1},{7,6},{6,5},{11,10},{10,9},{15,14},{14,13},{19,18},{18... | collective-permute-start | bytes 1966088 | tf_op jit(solution)/shard_map/ppermute | solution.py:422
  707.7 153.1 %reduce-scatter.14.cloned.1.call-start = ((), (), s32[]{:S(2)}) async-start(), calls=%async_computation.14 | async-start | bytes 5898240 | tf_op jit(solution)/shard_map/reduce_scatter | solution.py:521
  739.0 40.1 %collective-permute-start.62 = (bf16[1,128,2560]{2,1,0:T(8,128)(2,1)}, bf16[1,128,2560]{2,1,0:T(8,128)(2,1)}, u32[]{:S(2)}, u32[]{:S(2)}) collective-permute-start(bf16[1,128,2560]{2,1,0:T(8,128)(2,1)} %get-tuple-element.208), channel_id=1, source_target_pairs={{0,1},{1,2},{2,3},{4,5},{5,6},{6,7},{8,9},{9,10},{10,11},{12,13},{... | collective-permute-start | bytes 1966088 | tf_op jit(solution)/shard_map/ppermute | solution.py:422
  741.3 37.9 %collective-permute-start.63 = (bf16[1,128,2560]{2,1,0:T(8,128)(2,1)}, bf16[1,128,2560]{2,1,0:T(8,128)(2,1)}, u32[]{:S(2)}, u32[]{:S(2)}) collective-permute-start(bf16[1,128,2560]{2,1,0:T(8,128)(2,1)} %get-tuple-element.209), channel_id=1, source_target_pairs={{3,2},{2,1},{1,0},{7,6},{6,5},{5,4},{11,10},{10,9},{9,8},{15,14},{... | collective-permute-start | bytes 1966088 | tf_op jit(solution)/shard_map/ppermute | solution.py:422
  742.6 36.6 %collective-permute-start.64 = (bf16[1,128,2560]{2,1,0:T(8,128)(2,1)}, bf16[1,128,2560]{2,1,0:T(8,128)(2,1)S(1)}, u32[]{:S(2)}, u32[]{:S(2)}) collective-permute-start(bf16[1,128,2560]{2,1,0:T(8,128)(2,1)} %get-tuple-element.211), channel_id=1, source_target_pairs={{0,1},{1,2},{2,3},{4,5},{5,6},{6,7},{8,9},{9,10},{10,11},{12,13},{... | collective-permute-start | bytes 1966088 | tf_op jit(solution)/shard_map/ppermute | solution.py:422
  748.0 31.2 %collective-permute-start.65 = (bf16[1,128,2560]{2,1,0:T(8,128)(2,1)}, bf16[1,128,2560]{2,1,0:T(8,128)(2,1)}, u32[]{:S(2)}, u32[]{:S(2)}) collective-permute-start(bf16[1,128,2560]{2,1,0:T(8,128)(2,1)} %get-tuple-element.212), channel_id=1, source_target_pairs={{3,2},{2,1},{1,0},{7,6},{6,5},{5,4},{11,10},{10,9},{9,8},{15,14},{... | collective-permute-start | bytes 1966088 | tf_op jit(solution)/shard_map/ppermute | solution.py:422
  (165 other events, 2580.9 us)
Sparse Core Ops, SparseCore 0:
  13.0 43.6 all-gather.5
  58.6 37.1 all-gather.7
  97.7 60.2 all-gather.9
  159.7 57.5 all-gather.13
  219.0 57.5 all-gather.11
  402.1 80.3 reduce-scatter.5
  486.2 75.3 reduce-scatter.7
  565.2 79.5 reduce-scatter.9
  707.8 54.6 reduce-scatter.11
  774.7 66.0 reduce-scatter.13
